TPU v7x, 32 devices: a whole 2x2x4 slice. The times are simulated.
32 devices in a mesh: tp: 4 (over y, core), dp: 8 (over z, x).
Axes of the slice: x: 2, y: 2, z: 4, core: 2. Of those that a mesh axis runs over, the one named last changes fastest.
Arguments:
- teacher_query: bfloat16 [8192, 8192], P('dp', 'tp'), may hold values from -8 to 8
- student_hidden: bfloat16 [8192, 4096], P('dp', 'tp'), may hold values from -16 to 16
- query_weight: bfloat16 [4096, 4096], P('dp', 'tp'), may hold values from -0.039794922 to 0.039794922
Outputs:
- kl_rows: float32 [32, 8192], P(('tp', 'dp'))
- weight_grad: float32 [4096, 4096], P('dp', 'tp')
All inputs are finite; a program needn't handle non-finite values.
Results may differ from a plain program's by a relative error of at most 0.0029.
Values may be sent and summed in bfloat16 or wider, within the bound.
A program may use at most 64 MiB of HBM per device.

v0:
```python
import functools
import math

import jax
import jax.numpy as jnp
from jax import lax
from jax.experimental import pallas as pl
from jax.experimental.pallas import tpu as pltpu
from jax.sharding import PartitionSpec as P

RHEADS = 32
NSEQ = 2
SEQ = 4096


def spread_heads(queries, heads, copies):
    rows = queries.shape[0]
    width = queries.shape[1] // heads
    shaped = queries.reshape(rows, heads, 1, width)
    return jnp.broadcast_to(shaped, (rows, heads, copies, width)).reshape(
        rows, heads * copies, width
    )

LOG2E = 1.0 / math.log(2.0)
LN2 = math.log(2.0)
LANES = 128


def relation_body(
    t_rows, t_keys, s_rows, s_keys, s_rows_t, kl_out, grad_out, t_buf, s_buf, g_buf, row_acc, key_acc,
    *, group, chunk, t_scale, s_scale,
):
    step = pl.program_id(0)
    block = t_rows.shape[0]
    keys = t_keys.shape[0]
    nt = (((1,), (1,)), ((), ()))

    for c in range(keys // chunk):
        at = slice(c * chunk, (c + 1) * chunk)
        t_buf[:, at] = lax.dot_general(t_rows[...], t_keys[at, :], nt, preferred_element_type=jnp.float32)
        s_buf[:, at] = lax.dot_general(s_rows[...], s_keys[at, :], nt, preferred_element_type=jnp.float32)

    tiles = keys // LANES
    ct = t_scale * LOG2E
    cs = s_scale * LOG2E

    def rows_of(i, carry):
        at = pl.ds(pl.multiple_of(i * group, group), group)
        t_max = t_buf[at, 0:LANES]
        s_max = s_buf[at, 0:LANES]
        for k in range(1, tiles):
            cols = slice(k * LANES, (k + 1) * LANES)
            t_max = jnp.maximum(t_max, t_buf[at, cols])
            s_max = jnp.maximum(s_max, s_buf[at, cols])
        t_max = jnp.broadcast_to(jnp.max(t_max, axis=1, keepdims=True), (group, LANES))
        s_max = jnp.broadcast_to(jnp.max(s_max, axis=1, keepdims=True), (group, LANES))
        t_sum = jnp.zeros((group, LANES), jnp.float32)
        s_sum = jnp.zeros((group, LANES), jnp.float32)
        gap = jnp.zeros((group, LANES), jnp.float32)
        for k in range(tiles):
            cols = slice(k * LANES, (k + 1) * LANES)
            u = (t_buf[at, cols] - t_max) * ct
            v = (s_buf[at, cols] - s_max) * cs
            t_exp = jnp.exp2(u)
            s_exp = jnp.exp2(v)
            t_buf[at, cols] = t_exp
            s_buf[at, cols] = s_exp
            t_sum = t_sum + t_exp
            s_sum = s_sum + s_exp
            gap = gap + t_exp * (u - v)
        t_sum = jnp.sum(t_sum, axis=1, keepdims=True)
        s_sum = jnp.sum(s_sum, axis=1, keepdims=True)
        gap = jnp.sum(gap, axis=1, keepdims=True)
        kl = gap * LN2 / t_sum - jnp.log(t_sum) + jnp.log(s_sum)
        kl_out[0, at, :] = jnp.broadcast_to(kl, (group, LANES))
        t_inv = jnp.broadcast_to(1.0 / t_sum, (group, LANES))
        s_inv = jnp.broadcast_to(1.0 / s_sum, (group, LANES))
        for k in range(tiles):
            cols = slice(k * LANES, (k + 1) * LANES)
            g_buf[at, cols] = (s_buf[at, cols] * s_inv - t_buf[at, cols] * t_inv).astype(jnp.bfloat16)
        return carry

    lax.fori_loop(0, block // group, rows_of, 0)

    @pl.when(step == 0)
    def _():
        key_acc[...] = jnp.zeros_like(key_acc)

    row_acc[pl.ds(pl.multiple_of(step * block, block), block), :] = jnp.dot(
        g_buf[...], s_keys[...], preferred_element_type=jnp.float32
    )
    for c in range(keys // chunk):
        at = slice(c * chunk, (c + 1) * chunk)
        key_acc[:, at] += jnp.dot(s_rows_t[...], g_buf[:, at], preferred_element_type=jnp.float32)

    @pl.when(step == pl.num_programs(0) - 1)
    def _():
        def finish(c, carry):
            at = pl.ds(pl.multiple_of(c * LANES, LANES), LANES)
            grad_out[at, :] = ((row_acc[at, :] + key_acc[:, at].T) * s_scale).astype(jnp.bfloat16)
            return carry

        lax.fori_loop(0, keys // LANES, finish, 0)


def relation(teacher, student):
    keys, t_width = teacher.shape
    s_width = student.shape[1]
    block = min(256, keys)
    group = 16
    chunk = min(1024, keys)
    steps = keys // block
    kl, grad = pl.pallas_call(
        functools.partial(
            relation_body, group=group, chunk=chunk, t_scale=t_width ** (-0.5), s_scale=s_width ** (-0.5)
        ),
        grid=(steps,),
        in_specs=[
            pl.BlockSpec((block, t_width), lambda i: (i, 0)),
            pl.BlockSpec((keys, t_width), lambda i: (0, 0)),
            pl.BlockSpec((block, s_width), lambda i: (i, 0)),
            pl.BlockSpec((keys, s_width), lambda i: (0, 0)),
            pl.BlockSpec((s_width, block), lambda i: (0, i)),
        ],
        out_specs=[
            pl.BlockSpec((1, block, LANES), lambda i: (i, 0, 0)),
            pl.BlockSpec((keys, s_width), lambda i: (0, 0)),
        ],
        out_shape=[
            jax.ShapeDtypeStruct((steps, block, LANES), jnp.float32),
            jax.ShapeDtypeStruct((keys, s_width), jnp.bfloat16),
        ],
        scratch_shapes=[
            pltpu.VMEM((block, keys), jnp.float32),
            pltpu.VMEM((block, keys), jnp.float32),
            pltpu.VMEM((block, keys), jnp.bfloat16),
            pltpu.VMEM((keys, s_width), jnp.float32),
            pltpu.VMEM((s_width, keys), jnp.float32),
        ],
        compiler_params=pltpu.CompilerParams(
            dimension_semantics=("arbitrary",), vmem_limit_bytes=40 * 1024 * 1024
        ),
        name="relation",
    )(teacher, teacher, student, student, student.T)
    return kl[:, :, 0].reshape(keys), grad


def whole_heads(teacher_query, student_hidden, query_weight):
    width = teacher_query.shape[1] // lax.axis_size("dp")
    teacher_all = lax.all_to_all(teacher_query, "dp", split_axis=1, concat_axis=0, tiled=True)
    hidden_full = lax.all_gather(student_hidden, "tp", axis=1, tiled=True)
    weight_full = lax.all_gather(query_weight, "dp", axis=0, tiled=True)
    student_query = jnp.dot(hidden_full, weight_full, preferred_element_type=jnp.float32).astype(jnp.bfloat16)
    student_all = lax.all_to_all(student_query, "dp", split_axis=1, concat_axis=0, tiled=True)
    hidden_cols = lax.all_to_all(hidden_full, "dp", split_axis=1, concat_axis=0, tiled=True)
    kls = []
    total = None
    for s in range(NSEQ):
        at = slice(s * SEQ, (s + 1) * SEQ)
        kl, grad = relation(teacher_all[at], student_all[at])
        kls.append(kl)
        grads = lax.all_gather(grad, "dp", axis=1, tiled=True)
        part = lax.dot_general(
            hidden_cols[at], grads, (((0,), (0,)), ((), ())), preferred_element_type=jnp.float32
        )
        total = part if total is None else total + part
    return jnp.concatenate(kls).reshape(1, NSEQ * SEQ), total


def local(teacher_query, student_hidden, query_weight):
    heads_here = RHEADS // lax.axis_size("tp")
    copies = lax.axis_size("dp") // heads_here
    if copies == 1 and heads_here == lax.axis_size("dp"):
        return whole_heads(teacher_query, student_hidden, query_weight)
    rows = teacher_query.shape[0]
    teacher_width = teacher_query.shape[1] // heads_here
    hidden_full = lax.all_gather(student_hidden, "tp", axis=1, tiled=True)
    teacher_send = spread_heads(teacher_query, heads_here, copies)
    projected = jnp.dot(
        hidden_full,
        lax.all_gather(query_weight, "dp", axis=0, tiled=True),
        preferred_element_type=jnp.float32,
    )
    student_query = projected.astype(jnp.bfloat16)
    student_width = student_query.shape[1] // heads_here
    student_send = spread_heads(student_query, heads_here, copies)
    teacher_all, student_all = (
        lax.all_to_all(teacher_send, "dp", split_axis=1, concat_axis=0, tiled=True),
        lax.all_to_all(student_send, "dp", split_axis=1, concat_axis=0, tiled=True),
    )
    total_rows = teacher_all.shape[0]
    teacher_all = teacher_all.reshape(total_rows, teacher_width)
    student_all = student_all.reshape(total_rows, student_width)
    teacher_scale = teacher_width ** (-0.5)
    student_scale = student_width ** (-0.5)
    query_rows = SEQ // copies
    first_row = lax.axis_index("dp") % copies * query_rows
    block = min(512, query_rows)
    blocks_each = query_rows // block

    def relation_step(step, carry):
        kl_store, grad_store = carry
        sequence = step // blocks_each
        offset = step % blocks_each * block
        base = sequence * SEQ
        start = base + first_row + offset
        teacher_keys = lax.dynamic_slice_in_dim(teacher_all, base, SEQ, 0)
        student_keys = lax.dynamic_slice_in_dim(student_all, base, SEQ, 0)
        teacher_rows = lax.dynamic_slice_in_dim(teacher_all, start, block, 0)
        student_rows = lax.dynamic_slice_in_dim(student_all, start, block, 0)
        teacher_scores = (
            lax.dot_general(
                teacher_rows,
                teacher_keys,
                (((1,), (1,)), ((), ())),
                preferred_element_type=jnp.float32,
            )
            * teacher_scale
        )
        student_scores = (
            lax.dot_general(
                student_rows,
                student_keys,
                (((1,), (1,)), ((), ())),
                preferred_element_type=jnp.float32,
            )
            * student_scale
        )
        teacher_log = jax.nn.log_softmax(teacher_scores, axis=-1)
        student_log = jax.nn.log_softmax(student_scores, axis=-1)
        teacher_prob = jnp.exp(teacher_log)
        divergence = jnp.sum(teacher_prob * (teacher_log - student_log), axis=-1)
        score_grad = (jnp.exp(student_log) - teacher_prob).astype(jnp.bfloat16)
        key_part = (
            lax.dot_general(
                score_grad,
                student_rows,
                (((0,), (0,)), ((), ())),
                preferred_element_type=jnp.float32,
            )
            * student_scale
        )
        row_part = (
            jnp.dot(score_grad, student_keys, preferred_element_type=jnp.float32) * student_scale
        )
        seq_grad = lax.dynamic_slice_in_dim(grad_store, base, SEQ, 0)
        grad_store = lax.dynamic_update_slice_in_dim(grad_store, seq_grad + key_part, base, 0)
        current = lax.dynamic_slice_in_dim(grad_store, start, block, 0)
        grad_store = lax.dynamic_update_slice_in_dim(grad_store, current + row_part, start, 0)
        kl_store = lax.dynamic_update_slice_in_dim(
            kl_store, divergence, sequence * query_rows + offset, 0
        )
        return (kl_store, grad_store)

    kl_init = jnp.zeros((NSEQ * query_rows,), jnp.float32)
    grad_init = jnp.zeros((total_rows, student_width), jnp.float32)
    kl_store, grad_store = lax.fori_loop(0, NSEQ * blocks_each, relation_step, (kl_init, grad_init))
    returned = lax.all_to_all(
        grad_store.reshape(heads_here * copies, rows, student_width),
        "dp",
        split_axis=0,
        concat_axis=2,
        tiled=True,
    )
    summed = jnp.sum(returned.reshape(rows, heads_here, copies, student_width), axis=2)
    query_grad = summed.reshape(rows, heads_here * student_width).astype(jnp.bfloat16)
    weight_grad = lax.psum_scatter(
        lax.dot_general(
            hidden_full, query_grad, (((0,), (0,)), ((), ())), preferred_element_type=jnp.float32
        ),
        "dp",
        scatter_dimension=0,
        tiled=True,
    )
    return (kl_store.reshape(1, NSEQ * query_rows), weight_grad)


def solution(mesh):
    placed = (P("dp", "tp"), P("dp", "tp"), P("dp", "tp"))
    return jax.shard_map(
        local,
        mesh=mesh,
        in_specs=placed,
        out_specs=(P(("tp", "dp"), None), P("dp", "tp")),
        check_vma=False,
    )
```

profile of v0, /device:TPU:0, one launch (start us, length us, event | category | flops | bytes accessed | tf_op | source)
XLA Modules:
  0.0 845.9 jit_solution(13697044965763636197)
XLA Ops:
  7.2 0.0 all-gather.5.cloned.1.call-start
  7.2 3.9 copy.30
  11.2 0.0 all-gather.5.cloned.1.call-update
  11.2 0.0 all-gather.7.cloned.1.call-start
  11.2 0.7 all-gather.7.cloned.1.call-update
  11.9 4.5 copy.46
  16.4 7.3 all-to-all-start
  23.7 48.6 %all-gather.5.cloned.1.call-done = bf16[1024,4096]{0,1:T(8,128)(2,1)} async-done(((bf16[1024,1024]{0,1:T(8,128)(2,1)}), bf16[1024,4096]{0,1:T(8,128)(2,1)}) %all-gather.5.cloned.1.call-update) | async-done | bytes 8388624 | tf_op jit(solution)/shard_map/all_gather | solution.py:151
  72.3 151.5 %all-gather.7.cloned.1.call-done = bf16[4096,1024]{1,0:T(8,128)(2,1)} async-done(((bf16[512,1024]{1,0:T(8,128)(2,1)}), bf16[4096,1024]{1,0:T(8,128)(2,1)}) %all-gather.7.cloned.1.call-update) | async-done | bytes 8388624 | tf_op jit(solution)/shard_map/all_gather | solution.py:152
  223.8 14.7 %convolution_convert_fusion = bf16[1024,1024]{0,1:T(8,128)(2,1)} fusion(bf16[1024,4096]{0,1:T(8,128)(2,1)} %all-gather.5.cloned.1.call-done, bf16[4096,1024]{1,0:T(8,128)(2,1)} %all-gather.7.cloned.1.call-done), kind=kOutput, calls=%fused_computation.4 | convolution fusion | flops 8590983168 | bytes 18874368 | tf_op jit(solution)/shard_map/dot_general | solution.py:153
  238.5 0.0 all-to-all-done
  238.5 4.4 all-to-all-start.1
  242.9 0.0 all-gather.9.cloned.1.call-start
  242.9 3.8 fusion.1
  246.8 43.9 %all-to-all-done.1 = bf16[1024,8,128]{0,2,1:T(8,128)(2,1)} async-done(((bf16[1024,8,128]{0,2,1:T(8,128)(2,1)}), bf16[1024,8,128]{0,2,1:T(8,128)(2,1)}, u32[]{:S(2)}, u32[]{:S(2)}) %all-to-all-start.1) | async-done | bytes 2097184 | tf_op jit(solution)/shard_map/all_to_all | solution.py:154
  290.7 2.7 slice_bitcast_fusion.1
  293.4 1.1 copy.41
  294.5 1.6 copy.32.s_rows.s_keys
  296.1 0.0 copy-start
  296.1 1.6 copy-done
  297.7 1.2 copy-done.2
  298.9 122.9 %relation.2 = (f32[16,256,128]{2,1,0:T(8,128)S(1)}, bf16[4096,128]{1,0:T(8,128)(2,1)S(1)}) custom-call(bf16[4096,256]{1,0:T(8,128)(2,1)S(1)} %bitcast.38, bf16[4096,256]{1,0:T(8,128)(2,1)S(1)} %bitcast.39, bf16[4096,128]{1,0:T(8,128)(2,1)S(1)} %copy.32.s_rows.s_keys, bf16[4096,128]{1,0:T(8,128)(2,1)S(1)} %copy.32.s_rows.s_keys, bf16[128,4096]{1,0:T(8,128)(2,1)S(1)} %bitcast.43), custom_call_target="tpu_custom_call" | custom-call | tf_op jit(solution)/shard_map/relation/pallas_call | solution.py:113
  421.9 1.3 copy-done.3
  423.2 1.0 copy-done.6
  424.2 0.0 all-gather.9.cloned.1.call-update
  424.2 5.2 all-to-all-start.2
  429.4 0.2 all-gather.11.cloned.1.call-start
  429.6 1.1 copy.42
  430.7 1.7 copy.35.s_rows.s_keys
  432.4 0.0 copy-start.1
  432.4 1.3 copy-done.1
  433.7 122.9 %relation.3 = (f32[16,256,128]{2,1,0:T(8,128)S(1)}, bf16[4096,128]{1,0:T(8,128)(2,1)S(1)}) custom-call(bf16[4096,256]{1,0:T(8,128)(2,1)S(1)} %bitcast.36, bf16[4096,256]{1,0:T(8,128)(2,1)S(1)} %bitcast.37, bf16[4096,128]{1,0:T(8,128)(2,1)S(1)} %copy.35.s_rows.s_keys, bf16[4096,128]{1,0:T(8,128)(2,1)S(1)} %copy.35.s_rows.s_keys, bf16[128,4096]{1,0:T(8,128)(2,1)S(1)} %bitcast.41), custom_call_target="tpu_custom_call" | custom-call | tf_op jit(solution)/shard_map/relation/pallas_call | solution.py:113
  556.6 0.0 copy-start.5
  556.6 1.3 copy-done.5
  557.9 1.0 copy-done.7
  558.9 0.0 all-gather.11.cloned.1.call-update
  558.9 2.3 slice_reduce_fusion
  561.3 0.0 copy-done.4
  561.3 0.6 slice_reduce_fusion.1
  561.9 0.6 pad_maximum_fusion
  562.5 150.0 %all-to-all-done.2 = bf16[1024,8,512]{0,2,1:T(8,128)(2,1)} async-done(((bf16[1024,8,512]{0,2,1:T(8,128)(2,1)}), bf16[1024,8,512]{0,2,1:T(8,128)(2,1)}, u32[]{:S(2)}, u32[]{:S(2)}) %all-to-all-start.2) | async-done | bytes 8388640 | tf_op jit(solution)/shard_map/all_to_all | solution.py:155
  712.5 6.2 fusion
  718.7 6.3 copy.37
  725.0 6.2 copy.38
  731.2 10.4 %fusion.2 = f32[1024,512]{1,0:T(8,128)} fusion(bf16[4096,1024]{1,0:T(8,128)(2,1)} %all-gather.9.cloned.1.call-done, bf16[4096,512]{1,0:T(8,128)(2,1)} %bitcast.48), kind=kOutput, calls=%fused_computation.10 | convolution fusion | flops 4294967296 | bytes 14680064 | tf_op jit(solution)/shard_map/dot_general | solution.py:163
  741.6 86.2 %all-gather.11.cloned.1.call-done = bf16[4096,1024]{1,0:T(8,128)(2,1)} async-done(((bf16[4096,128]{1,0:T(8,128)(2,1)}), bf16[4096,1024]{1,0:T(8,128)(2,1)}) %all-gather.11.cloned.1.call-update) | async-done | bytes 8388624 | tf_op jit(solution)/shard_map/all_gather | solution.py:162
  827.8 9.8 %add_bitcast_fusion = f32[512,1024]{0,1:T(8,128)S(1)} fusion(f32[1024,512]{1,0:T(8,128)} %fusion.2, bf16[4096,1024]{1,0:T(8,128)(2,1)} %all-gather.11.cloned.1.call-done, bf16[4096,512]{1,0:T(8,128)(2,1)} %bitcast.47), kind=kOutput, calls=%fused_computation.1 | convolution fusion | flops 4295491584 | bytes 16777216 | tf_op jit(solution)/shard_map/dot_general | solution.py:163
  837.6 1.8 copy.39
  (10 shorter events, 0.0 us)
Async XLA Ops:
  7.2 65.2 %all-gather.5.cloned.1.call-start = ((), (), s32[]{:S(2)}) async-start(), calls=%async_computation.3 | async-start | bytes 10485760 | tf_op jit(solution)/shard_map/all_gather | solution.py:151
  11.2 212.6 %all-gather.7.cloned.1.call-start = ((), (), s32[]{:S(2)}) async-start(), calls=%async_computation.4 | async-start | bytes 9437184 | tf_op jit(solution)/shard_map/all_gather | solution.py:152
  16.4 222.1 %all-to-all-start = ((bf16[1024,8,256]{2,0,1:T(8,128)(2,1)}), bf16[1024,8,256]{2,0,1:T(8,128)(2,1)}, u32[]{:S(2)}, u32[]{:S(2)}) async-start(bf16[1024,8,256]{2,0,1:T(8,128)(2,1)} %bitcast.44), calls=%async_computation | async-start | bytes 8388608 | tf_op jit(solution)/shard_map/all_to_all | solution.py:150
  238.5 52.2 %all-to-all-start.1 = ((bf16[1024,8,128]{0,2,1:T(8,128)(2,1)}), bf16[1024,8,128]{0,2,1:T(8,128)(2,1)}, u32[]{:S(2)}, u32[]{:S(2)}) async-start(bf16[1024,8,128]{0,2,1:T(8,128)(2,1)} %bitcast.2), calls=%async_computation.1 | async-start | bytes 4194304 | tf_op jit(solution)/shard_map/all_to_all | solution.py:154
  242.9 488.3 %all-gather.9.cloned.1.call-start = ((), (), s32[]{:S(2)}) async-start(), calls=%async_computation.5 | async-start | bytes 9437184 | tf_op jit(solution)/shard_map/all_gather | solution.py:162
  296.1 1.6 copy-start
  297.7 1.2 copy-start.2
  421.9 1.3 copy-start.3
  423.2 1.0 copy-start.6
  424.2 5.4 copy-start.8
  424.2 288.3 %all-to-all-start.2 = ((bf16[1024,8,512]{0,2,1:T(8,128)(2,1)}), bf16[1024,8,512]{0,2,1:T(8,128)(2,1)}, u32[]{:S(2)}, u32[]{:S(2)}) async-start(bf16[1024,8,512]{0,2,1:T(8,128)(2,1)} %bitcast.45), calls=%async_computation.2 | async-start | bytes 16777216 | tf_op jit(solution)/shard_map/all_to_all | solution.py:155
  429.4 398.4 %all-gather.11.cloned.1.call-start = ((), (), s32[]{:S(2)}) async-start(), calls=%async_computation.6 | async-start | bytes 9437184 | tf_op jit(solution)/shard_map/all_gather | solution.py:162
  432.4 1.3 copy-start.1
  556.6 1.3 copy-start.5
  557.9 1.0 copy-start.7
  558.9 2.4 copy-start.4
Sparse Core Ops, SparseCore 0:
  11.3 60.9 all-gather.4
  74.4 149.3 all-gather.6
  424.3 278.3 all-gather.8
  704.6 123.1 all-gather.10
where the time goes:
time: 847 us; the launch traced here: 846 us
  waiting for transfers between devices  481 us (57%)
  Pallas kernels  246 us (29%)
  local copies, waits for them, and re-layouts  52.6 us (6%)
  matrix products  34.9 us (4%)
  starting transfers between devices  17.2 us (2%)
  between operations  13.9 us (2%)
    pallas_call x2, Pallas kernels, relation(): pl.pallas_call(functools.partial(relation_body, group=group, chunk=chunk,...  246 us
    all_gather x1, waiting for transfers between devices, whole_heads(): weight_full = lax.all_gather(query_weight, 'dp', axis=0, tiled=True)  151 us
    all_to_all x1, waiting for transfers between devices, whole_heads(): lax.all_to_all(hidden_full, 'dp', split_axis=1, concat_axis=0, tiled=True)  150 us
    all_gather x2, waiting for transfers between devices, whole_heads(): grads = lax.all_gather(grad, 'dp', axis=1, tiled=True)  86.2 us
    all_gather x1, waiting for transfers between devices, whole_heads(): hidden_full = lax.all_gather(student_hidden, 'tp', axis=1, tiled=True)  48.6 us
    all_to_all x1, waiting for transfers between devices, whole_heads(): lax.all_to_all(student_query, 'dp', split_axis=1, concat_axis=0, tiled=True)  43.9 us
    dot_general x2, matrix products, whole_heads(): lax.dot_general(hidden_cols[at], grads, (((0,), (0,)), ((), ())), preferr...  20.2 us
    slice x3, local copies, waits for them, and re-layouts, whole_heads(): hidden_cols[at]  18.7 us
  transfers between devices with their start and end apart: 7, of which 5 were waited for; matrix products, arithmetic and copies ran while one was open for 7% of the time, Pallas kernels for 15%

commit v1 on v0

--- a/solution.py
+++ b/solution.py
@@ -103,9 +103,10 @@
         lax.fori_loop(0, keys // LANES, finish, 0)
 
 
-def relation(teacher, student):
-    keys, t_width = teacher.shape
-    s_width = student.shape[1]
+def relation(teacher, student, part, parts):
+    keys = teacher.shape[0]
+    t_width = teacher.shape[1] // parts
+    s_width = student.shape[1] // parts
     block = min(256, keys)
     group = 16
     chunk = min(1024, keys)
@@ -116,11 +117,11 @@
         ),
         grid=(steps,),
         in_specs=[
-            pl.BlockSpec((block, t_width), lambda i: (i, 0)),
-            pl.BlockSpec((keys, t_width), lambda i: (0, 0)),
-            pl.BlockSpec((block, s_width), lambda i: (i, 0)),
-            pl.BlockSpec((keys, s_width), lambda i: (0, 0)),
-            pl.BlockSpec((s_width, block), lambda i: (0, i)),
+            pl.BlockSpec((block, t_width), lambda i: (i, part)),
+            pl.BlockSpec((keys, t_width), lambda i: (0, part)),
+            pl.BlockSpec((block, s_width), lambda i: (i, part)),
+            pl.BlockSpec((keys, s_width), lambda i: (0, part)),
+            pl.BlockSpec((s_width, block), lambda i: (part, i)),
         ],
         out_specs=[
             pl.BlockSpec((1, block, LANES), lambda i: (i, 0, 0)),
@@ -145,33 +146,44 @@
     return kl[:, :, 0].reshape(keys), grad
 
 
-def whole_heads(teacher_query, student_hidden, query_weight):
-    width = teacher_query.shape[1] // lax.axis_size("dp")
-    teacher_all = lax.all_to_all(teacher_query, "dp", split_axis=1, concat_axis=0, tiled=True)
+def heads_of_one_sequence(teacher_query, student_hidden, query_weight):
+    members = lax.axis_size("dp") // NSEQ
+    mine = RHEADS // lax.axis_size("tp") // members
+    groups = [[s * members + k for k in range(members)] for s in range(NSEQ)]
+    to_heads = functools.partial(
+        lax.all_to_all, axis_name="dp", split_axis=1, concat_axis=0, axis_index_groups=groups, tiled=True
+    )
+    teacher_all = to_heads(teacher_query)
     hidden_full = lax.all_gather(student_hidden, "tp", axis=1, tiled=True)
     weight_full = lax.all_gather(query_weight, "dp", axis=0, tiled=True)
     student_query = jnp.dot(hidden_full, weight_full, preferred_element_type=jnp.float32).astype(jnp.bfloat16)
-    student_all = lax.all_to_all(student_query, "dp", split_axis=1, concat_axis=0, tiled=True)
-    hidden_cols = lax.all_to_all(hidden_full, "dp", split_axis=1, concat_axis=0, tiled=True)
-    kls = []
-    total = None
-    for s in range(NSEQ):
-        at = slice(s * SEQ, (s + 1) * SEQ)
-        kl, grad = relation(teacher_all[at], student_all[at])
-        kls.append(kl)
-        grads = lax.all_gather(grad, "dp", axis=1, tiled=True)
-        part = lax.dot_general(
-            hidden_cols[at], grads, (((0,), (0,)), ((), ())), preferred_element_type=jnp.float32
-        )
-        total = part if total is None else total + part
-    return jnp.concatenate(kls).reshape(1, NSEQ * SEQ), total
+    student_all = to_heads(student_query)
+    rows_of = [0.0] * NSEQ
+    grads = []
+    for m in range(mine):
+        kl, grad = relation(teacher_all, student_all, m, mine)
+        for s in range(NSEQ):
+            pairs = [(s * members + k, k * mine + m) for k in range(members)]
+            rows_of[s] = rows_of[s] + lax.ppermute(kl, "dp", pairs)
+        part = lax.all_to_all(
+            grad, "dp", split_axis=0, concat_axis=1, axis_index_groups=groups, tiled=True
+        )
+        grads.append(part.reshape(part.shape[0], members, 1, part.shape[1] // members))
+    grad_rows = jnp.concatenate(grads, axis=2).reshape(student_query.shape)
+    partial = lax.dot_general(
+        hidden_full, grad_rows, (((0,), (0,)), ((), ())), preferred_element_type=jnp.float32
+    )
+    size = lax.axis_size("dp")
+    pieces = partial.reshape(size, partial.shape[0] // size, partial.shape[1]).astype(jnp.bfloat16)
+    landed = lax.all_to_all(pieces, "dp", split_axis=0, concat_axis=0, tiled=True)
+    return jnp.concatenate(rows_of).reshape(1, NSEQ * SEQ), jnp.sum(landed.astype(jnp.float32), axis=0)
 
 
 def local(teacher_query, student_hidden, query_weight):
     heads_here = RHEADS // lax.axis_size("tp")
     copies = lax.axis_size("dp") // heads_here
-    if copies == 1 and heads_here == lax.axis_size("dp"):
-        return whole_heads(teacher_query, student_hidden, query_weight)
+    if lax.axis_size("dp") % NSEQ == 0 and heads_here % (lax.axis_size("dp") // NSEQ) == 0:
+        return heads_of_one_sequence(teacher_query, student_hidden, query_weight)
     rows = teacher_query.shape[0]
     teacher_width = teacher_query.shape[1] // heads_here
     hidden_full = lax.all_gather(student_hidden, "tp", axis=1, tiled=True)

time: 847 us -> 795 us (0.939)
  waiting for transfers between devices: 481 us -> 424 us
  local copies, waits for them, and re-layouts: 52.6 us -> 29 us
  blocking collectives: 0 us -> 16.6 us
    ppermute x0 -> x4, waiting for transfers between devices: none -> 172 us  [heads_of_one_sequence(): rows_of[s] = rows_of[s] + lax.ppermute(kl, 'dp', pairs)]
    all_to_all x3 -> x4, waiting for transfers between devices: 194 us -> 62.5 us  [the longest x1 42.6 us: heads_of_one_sequence(): teacher_all = to_heads(teacher_query)]
    all_gather x4 -> x2, waiting for transfers between devices: 286 us -> 189 us  [the longest x1 127 us: heads_of_one_sequence(): weight_full = lax.all_gather(query_weight, 'dp', axis=0, tiled=True)]
    slice x8 -> x0, local copies, waits for them, and re-layouts: 28 us -> none  [the longest x3 18.7 us: whole_heads(): hidden_cols[at]]
    all_to_all x0 -> x1, blocking collectives: none -> 16.6 us  [heads_of_one_sequence(): lax.all_to_all(grad, 'dp', split_axis=0, concat_axis=1, axis_index_groups...]
    unnamed x23 -> x13, local copies, waits for them, and re-layouts: 17.1 us -> 7.65 us
    dot_general x3 -> x2, matrix products: 34.9 us -> 28.9 us  [the longest x1 14.7 us: heads_of_one_sequence(): jnp.dot(hidden_full, weight_full, preferred_element_type=jnp.float32)]
    all_to_all x3 -> x4, starting transfers between devices: 16.8 us -> 18.1 us  [the longest x1 5.16 us: heads_of_one_sequence(): lax.all_to_all(pieces, 'dp', split_axis=0, concat_axis=0, tiled=True)]
  transfers between devices with their start and end apart: 7 -> 10, of which waited for: 5 -> 6; matrix products, arithmetic and copies ran while one was open for 7% -> 2% of each run, Pallas kernels for 15% -> 16%
where the time goes in v1:
time: 795 us; the launch traced here: 794 us
  waiting for transfers between devices  424 us (53%)
  Pallas kernels  250 us (31%)
  local copies, waits for them, and re-layouts  29 us (4%)
  matrix products  28.9 us (4%)
  starting transfers between devices  24.6 us (3%)
  blocking collectives  16.6 us (2%)
  between operations  14.2 us (2%)
    pallas_call x2, Pallas kernels, relation(): pl.pallas_call(functools.partial(relation_body, group=group, chunk=chunk,...  250 us
    ppermute x4, waiting for transfers between devices, heads_of_one_sequence(): rows_of[s] = rows_of[s] + lax.ppermute(kl, 'dp', pairs)  172 us
    all_gather x1, waiting for transfers between devices, heads_of_one_sequence(): weight_full = lax.all_gather(query_weight, 'dp', axis=0, tiled=True)  127 us
    all_gather x1, waiting for transfers between devices, heads_of_one_sequence(): hidden_full = lax.all_gather(student_hidden, 'tp', axis=1, tiled=True)  61.9 us
    all_to_all x1, waiting for transfers between devices, heads_of_one_sequence(): teacher_all = to_heads(teacher_query)  42.6 us
    all_to_all x1, waiting for transfers between devices, heads_of_one_sequence(): student_all = to_heads(student_query)  19.9 us
    all_to_all x1, blocking collectives, heads_of_one_sequence(): lax.all_to_all(grad, 'dp', split_axis=0, concat_axis=1, axis_index_groups...  16.6 us
  transfers between devices with their start and end apart: 10, of which 6 were waited for; matrix products, arithmetic and copies ran while one was open for 2% of the time, Pallas kernels for 16%

profile of v1, /device:TPU:0, one launch (start us, length us, event | category | flops | bytes accessed | tf_op | source)
XLA Modules:
  0.0 794.2 jit_solution(5275053541828136263)
XLA Ops:
  7.2 0.0 all-gather.3.cloned.1.call-start
  7.2 0.7 all-gather.3.cloned.1.call-update
  7.9 0.0 all-gather.5.cloned.1.call-start
  7.9 0.7 all-gather.5.cloned.1.call-update
  8.6 61.9 %all-gather.3.cloned.1.call-done = bf16[1024,4096]{1,0:T(8,128)(2,1)} async-done(((bf16[1024,1024]{1,0:T(8,128)(2,1)}), bf16[1024,4096]{1,0:T(8,128)(2,1)}) %all-gather.3.cloned.1.call-update) | async-done | bytes 8388624 | tf_op jit(solution)/shard_map/all_gather | solution.py:157
  70.6 126.6 %all-gather.5.cloned.1.call-done = bf16[4096,1024]{1,0:T(8,128)(2,1)} async-done(((bf16[512,1024]{1,0:T(8,128)(2,1)}), bf16[4096,1024]{1,0:T(8,128)(2,1)}) %all-gather.5.cloned.1.call-update) | async-done | bytes 8388624 | tf_op jit(solution)/shard_map/all_gather | solution.py:158
  197.2 14.7 %convolution_convert_fusion.1 = bf16[1024,1024]{0,1:T(8,128)(2,1)} fusion(bf16[1024,4096]{1,0:T(8,128)(2,1)} %all-gather.3.cloned.1.call-done, bf16[4096,1024]{1,0:T(8,128)(2,1)} %all-gather.5.cloned.1.call-done), kind=kOutput, calls=%fused_computation.7 | convolution fusion | flops 8590983168 | bytes 18874368 | tf_op jit(solution)/shard_map/dot_general | solution.py:159
  211.9 3.6 all-to-all-start.1
  215.5 4.5 copy.39
  220.0 19.9 %all-to-all-done.1 = bf16[1024,4,256]{0,2,1:T(8,128)(2,1)S(1)} async-done(((bf16[1024,4,256]{0,2,1:T(8,128)(2,1)}), bf16[1024,4,256]{0,2,1:T(8,128)(2,1)S(1)}, u32[]{:S(2)}, u32[]{:S(2)}) %all-to-all-start.1) | async-done | bytes 2097184 | tf_op jit(solution)/shard_map/all_to_all | solution.py:160
  239.9 4.9 all-to-all-start
  244.8 1.6 copy.33
  246.4 3.3 copy.21.s_rows.s_keys
  249.7 42.6 %all-to-all-done = bf16[1024,4,512]{2,0,1:T(8,128)(2,1)} async-done(((bf16[1024,4,512]{2,0,1:T(8,128)(2,1)}), bf16[1024,4,512]{2,0,1:T(8,128)(2,1)}, u32[]{:S(2)}, u32[]{:S(2)}) %all-to-all-start) | async-done | bytes 4194336 | tf_op jit(solution)/shard_map/all_to_all | solution.py:156
  292.3 0.0 copy-start
  292.3 1.6 copy-done
  293.9 125.0 %relation.3 = (f32[16,256,128]{2,1,0:T(8,128)S(1)}, bf16[4096,128]{1,0:T(8,128)(2,1)S(1)}) custom-call(bf16[4096,512]{1,0:T(8,128)(2,1)} %bitcast.1.t_rows.t_keys, bf16[4096,512]{1,0:T(8,128)(2,1)} %bitcast.1.t_rows.t_keys, bf16[4096,256]{1,0:T(8,128)(2,1)S(1)} %copy.21.s_rows.s_keys, bf16[4096,256]{1,0:T(8,128)(2,1)S(1)} %copy.21.s_rows.s_keys, ...), custom_call_target="tpu_custom_call" | custom-call | tf_op jit(solution)/shard_map/relation/pallas_call | solution.py:114
  418.9 0.0 copy-start.2
  418.9 1.3 copy-done.2
  420.2 1.3 copy.26
  421.5 4.4 all-to-all-start.3
  426.0 0.0 copy-start.1
  426.0 1.6 copy-done.1
  427.6 124.9 %relation.2 = (f32[16,256,128]{2,1,0:T(8,128)S(1)}, bf16[4096,128]{1,0:T(8,128)(2,1)S(1)}) custom-call(bf16[4096,512]{1,0:T(8,128)(2,1)} %bitcast.1.t_rows.t_keys, bf16[4096,512]{1,0:T(8,128)(2,1)} %bitcast.1.t_rows.t_keys, bf16[4096,256]{1,0:T(8,128)(2,1)S(1)} %copy.21.s_rows.s_keys, bf16[4096,256]{1,0:T(8,128)(2,1)S(1)} %copy.21.s_rows.s_keys, ...), custom_call_target="tpu_custom_call" | custom-call | tf_op jit(solution)/shard_map/relation/pallas_call | solution.py:114
  552.5 0.0 copy-start.4
  552.5 1.3 copy-done.4
  553.8 0.5 copy.25
  554.4 0.0 all-to-all-done.3
  554.4 16.6 %all_to_all.75 = bf16[4,1024,128]{1,2,0:T(8,128)(2,1)S(1)} all-to-all(bf16[4,1024,128]{1,2,0:T(8,128)(2,1)S(1)} %copy.25), channel_id=1, replica_groups={{0,1,2,3},{4,5,6,7},{8,9,10,11},{12,13,14,15},{16,17,18,19},{20,21,22,2..., dimensions={0} | all-to-all | bytes 2097152 | tf_op jit(solution)/shard_map/all_to_all | solution.py:168
  571.0 1.4 pad_maximum_fusion
  572.4 14.2 %convolution_convert_fusion = bf16[1024,4096]{1,0:T(8,128)(2,1)} fusion(bf16[1024,1024]{0,1:T(8,128)(2,1)S(1)} %bitcast.48, bf16[1024,4096]{1,0:T(8,128)(2,1)} %all-gather.3.cloned.1.call-done), kind=kOutput, calls=%fused_computation.2 | convolution fusion | flops 8594128896 | bytes 18874368 | tf_op jit(solution)/shard_map/dot_general | solution.py:173
  586.6 7.4 copy.38
  594.0 5.2 all-to-all-start.4
  599.2 0.0 copy-done.3
  599.2 0.6 slice_reduce_fusion
  599.8 3.8 collective-permute-start.1
  603.6 2.2 slice_reduce_fusion.1
  605.8 0.7 collective-permute-start
  606.5 0.7 collective-permute-start.3
  607.2 1.3 collective-permute-start.2
  608.5 57.0 %collective-permute-done.1 = f32[4096]{0:T(1024)S(1)} collective-permute-done((f32[4096]{0:T(1024)S(1)}, f32[4096]{0:T(1024)S(1)}, u32[]{:S(2)}, u32[]{:S(2)}) %collective-permute-start.1) | collective-permute-done | bytes 16416 | tf_op jit(solution)/shard_map/ppermute | solution.py:167
  665.5 0.0 collective-permute-done
  665.5 0.0 collective-permute-done.3
  665.5 114.6 %collective-permute-done.2 = f32[4096]{0:T(1024)S(1)} collective-permute-done((f32[4096]{0:T(1024)S(1)}, f32[4096]{0:T(1024)S(1)}, u32[]{:S(2)}, u32[]{:S(2)}) %collective-permute-start.2) | collective-permute-done | bytes 16416 | tf_op jit(solution)/shard_map/ppermute | solution.py:167
  780.1 0.6 pad_maximum_fusion.1
  780.8 0.0 all-to-all-done.4
  780.8 4.8 convert_reduce_fusion
  785.5 1.8 copy.29
  (5 shorter events, 0.0 us)
Async XLA Ops:
  7.2 63.4 %all-gather.3.cloned.1.call-start = ((), (), s32[]{:S(2)}) async-start(), calls=%async_computation.5 | async-start | bytes 10485760 | tf_op jit(solution)/shard_map/all_gather | solution.py:157
  7.9 189.3 %all-gather.5.cloned.1.call-start = ((), (), s32[]{:S(2)}) async-start(), calls=%async_computation.6 | async-start | bytes 9437184 | tf_op jit(solution)/shard_map/all_gather | solution.py:158
  211.9 28.0 %all-to-all-start.1 = ((bf16[1024,4,256]{0,2,1:T(8,128)(2,1)}), bf16[1024,4,256]{0,2,1:T(8,128)(2,1)S(1)}, u32[]{:S(2)}, u32[]{:S(2)}) async-start(bf16[1024,4,256]{0,2,1:T(8,128)(2,1)} %bitcast.47), calls=%async_computation.1 | async-start | bytes 4194304 | tf_op jit(solution)/shard_map/all_to_all | solution.py:160
  239.9 52.4 %all-to-all-start = ((bf16[1024,4,512]{2,0,1:T(8,128)(2,1)}), bf16[1024,4,512]{2,0,1:T(8,128)(2,1)}, u32[]{:S(2)}, u32[]{:S(2)}) async-start(bf16[1024,4,512]{2,0,1:T(8,128)(2,1)} %bitcast.42), calls=%async_computation | async-start | bytes 8388608 | tf_op jit(solution)/shard_map/all_to_all | solution.py:156
  292.3 1.6 copy-start
  418.9 1.3 copy-start.2
  421.5 132.8 %all-to-all-start.3 = ((bf16[4,1024,128]{1,2,0:T(8,128)(2,1)}), bf16[4,1024,128]{1,2,0:T(8,128)(2,1)}, u32[]{:S(2)}, u32[]{:S(2)}) async-start(bf16[4,1024,128]{1,2,0:T(8,128)(2,1)} %copy.26), calls=%async_computation.3 | async-start | bytes 2097152 | tf_op jit(solution)/shard_map/all_to_all | solution.py:168
  426.0 1.6 copy-start.1
  552.5 1.3 copy-start.4
  594.0 5.2 copy-start.3
  594.0 186.8 %all-to-all-start.4 = ((bf16[8,512,1024]{1,2,0:T(8,128)(2,1)}), bf16[8,512,1024]{1,2,0:T(8,128)(2,1)}, u32[]{:S(2)}, u32[]{:S(2)}) async-start(bf16[8,512,1024]{1,2,0:T(8,128)(2,1)} %bitcast.41), calls=%async_computation.4 | async-start | bytes 16777216 | tf_op jit(solution)/shard_map/all_to_all | solution.py:178
  599.8 65.7 %collective-permute-start.1 = (f32[4096]{0:T(1024)S(1)}, f32[4096]{0:T(1024)S(1)}, u32[]{:S(2)}, u32[]{:S(2)}) collective-permute-start(f32[4096]{0:T(1024)S(1)} %bitcast.52), channel_id=1, source_target_pairs={{0,1},{1,3},{2,5},{3,7},{8,9},{9,11},{10,13},{11,15},{16,17},{17,1... | collective-permute-start | bytes 49160 | tf_op jit(solution)/shard_map/ppermute | solution.py:167
  605.8 59.7 %collective-permute-start = (f32[4096]{0:T(1024)S(1)}, f32[4096]{0:T(1024)S(1)}, u32[]{:S(2)}, u32[]{:S(2)}) collective-permute-start(f32[4096]{0:T(1024)S(1)} %bitcast.54), channel_id=1, source_target_pairs={{0,0},{1,2},{2,4},{3,6},{8,8},{9,10},{10,12},{11,14},{16,16},{17,1... | collective-permute-start | bytes 49160 | tf_op jit(solution)/shard_map/ppermute | solution.py:167
  606.5 59.0 %collective-permute-start.3 = (f32[4096]{0:T(1024)S(1)}, f32[4096]{0:T(1024)S(1)}, u32[]{:S(2)}, u32[]{:S(2)}) collective-permute-start(f32[4096]{0:T(1024)S(1)} %bitcast.53), channel_id=1, source_target_pairs={{4,1},{5,3},{6,5},{7,7},{12,9},{13,11},{14,13},{15,15},{20,17},{21... | collective-permute-start | bytes 49160 | tf_op jit(solution)/shard_map/ppermute | solution.py:167
  607.2 173.0 %collective-permute-start.2 = (f32[4096]{0:T(1024)S(1)}, f32[4096]{0:T(1024)S(1)}, u32[]{:S(2)}, u32[]{:S(2)}) collective-permute-start(f32[4096]{0:T(1024)S(1)} %bitcast.55), channel_id=1, source_target_pairs={{4,0},{5,2},{6,4},{7,6},{12,8},{13,10},{14,12},{15,14},{20,16},{21... | collective-permute-start | bytes 49160 | tf_op jit(solution)/shard_map/ppermute | solution.py:167
Sparse Core Ops, SparseCore 0:
  9.5 60.9 all-gather.2
  72.7 124.4 all-gather.4

commit v2 on v1

--- a/solution.py
+++ b/solution.py
@@ -26,45 +26,50 @@
 LANES = 128
 
 
-def relation_body(
-    t_rows, t_keys, s_rows, s_keys, s_rows_t, kl_out, grad_out, t_buf, s_buf, g_buf, row_acc, key_acc,
-    *, group, chunk, t_scale, s_scale,
-):
-    step = pl.program_id(0)
-    block = t_rows.shape[0]
-    keys = t_keys.shape[0]
-    nt = (((1,), (1,)), ((), ()))
-
-    for c in range(keys // chunk):
-        at = slice(c * chunk, (c + 1) * chunk)
-        t_buf[:, at] = lax.dot_general(t_rows[...], t_keys[at, :], nt, preferred_element_type=jnp.float32)
-        s_buf[:, at] = lax.dot_general(s_rows[...], s_keys[at, :], nt, preferred_element_type=jnp.float32)
-
+NT = (((1,), (1,)), ((), ()))
+
+
+def stage(t_keys, s_keys, s_turned, kl_out, t_new, s_new, t_old, s_old, g_new, g_old, exps, row_acc, key_acc,
+          *, score_row, grad_row, group, t_scale, s_scale):
+    block, keys = t_new.shape
+    groups = block // group
+    pieces = groups // 2
+    chunk = keys // pieces
     tiles = keys // LANES
     ct = t_scale * LOG2E
     cs = s_scale * LOG2E
-
-    def rows_of(i, carry):
-        at = pl.ds(pl.multiple_of(i * group, group), group)
-        t_max = t_buf[at, 0:LANES]
-        s_max = s_buf[at, 0:LANES]
+    rows = pl.ds(pl.multiple_of(score_row, block), block)
+    old_rows = pl.ds(pl.multiple_of(grad_row, block), block)
+
+    def rows_at(i):
+        return pl.ds(pl.multiple_of(i * group, group), group)
+
+    def tops(i):
+        at = rows_at(i)
+        t_max = t_old[at, 0:LANES]
+        s_max = s_old[at, 0:LANES]
         for k in range(1, tiles):
-            cols = slice(k * LANES, (k + 1) * LANES)
-            t_max = jnp.maximum(t_max, t_buf[at, cols])
-            s_max = jnp.maximum(s_max, s_buf[at, cols])
-        t_max = jnp.broadcast_to(jnp.max(t_max, axis=1, keepdims=True), (group, LANES))
-        s_max = jnp.broadcast_to(jnp.max(s_max, axis=1, keepdims=True), (group, LANES))
+            c = slice(k * LANES, (k + 1) * LANES)
+            t_max = jnp.maximum(t_max, t_old[at, c])
+            s_max = jnp.maximum(s_max, s_old[at, c])
+        return (
+            jnp.broadcast_to(jnp.max(t_max, axis=1, keepdims=True), (group, LANES)),
+            jnp.broadcast_to(jnp.max(s_max, axis=1, keepdims=True), (group, LANES)),
+        )
+
+    def sums(i, t_max, s_max, t_e, s_e):
+        at = rows_at(i)
         t_sum = jnp.zeros((group, LANES), jnp.float32)
         s_sum = jnp.zeros((group, LANES), jnp.float32)
         gap = jnp.zeros((group, LANES), jnp.float32)
         for k in range(tiles):
-            cols = slice(k * LANES, (k + 1) * LANES)
-            u = (t_buf[at, cols] - t_max) * ct
-            v = (s_buf[at, cols] - s_max) * cs
+            c = slice(k * LANES, (k + 1) * LANES)
+            u = (t_old[at, c] - t_max) * ct
+            v = (s_old[at, c] - s_max) * cs
             t_exp = jnp.exp2(u)
             s_exp = jnp.exp2(v)
-            t_buf[at, cols] = t_exp
-            s_buf[at, cols] = s_exp
+            t_e[:, c] = t_exp
+            s_e[:, c] = s_exp
             t_sum = t_sum + t_exp
             s_sum = s_sum + s_exp
             gap = gap + t_exp * (u - v)
@@ -73,103 +78,363 @@
         gap = jnp.sum(gap, axis=1, keepdims=True)
         kl = gap * LN2 / t_sum - jnp.log(t_sum) + jnp.log(s_sum)
         kl_out[0, at, :] = jnp.broadcast_to(kl, (group, LANES))
-        t_inv = jnp.broadcast_to(1.0 / t_sum, (group, LANES))
-        s_inv = jnp.broadcast_to(1.0 / s_sum, (group, LANES))
+        return jnp.broadcast_to(1.0 / t_sum, (group, LANES)), jnp.broadcast_to(1.0 / s_sum, (group, LANES))
+
+    def score_grads(i, t_inv, s_inv, t_e, s_e):
+        at = rows_at(i)
         for k in range(tiles):
-            cols = slice(k * LANES, (k + 1) * LANES)
-            g_buf[at, cols] = (s_buf[at, cols] * s_inv - t_buf[at, cols] * t_inv).astype(jnp.bfloat16)
-        return carry
-
-    lax.fori_loop(0, block // group, rows_of, 0)
-
-    @pl.when(step == 0)
+            c = slice(k * LANES, (k + 1) * LANES)
+            g_new[at, c] = (s_e[:, c] * s_inv - t_e[:, c] * t_inv).astype(jnp.bfloat16)
+
+    def matmuls(i):
+        half = chunk // 2
+        for h in range(2):
+            cols = pl.ds(pl.multiple_of(i * chunk + h * half, half), half)
+            t_new[:, cols] = lax.dot_general(t_keys[rows, :], t_keys[cols, :], NT, preferred_element_type=jnp.float32)
+            s_new[:, cols] = lax.dot_general(s_keys[rows, :], s_keys[cols, :], NT, preferred_element_type=jnp.float32)
+            key_acc[:, cols] += jnp.dot(s_turned[:, old_rows], g_old[:, cols], preferred_element_type=jnp.float32)
+        cols = pl.ds(pl.multiple_of(i * chunk, chunk), chunk)
+        row_acc[:, old_rows] += lax.dot_general(
+            s_turned[:, cols], g_old[:, cols], NT, preferred_element_type=jnp.float32
+        )
+
+    t_even, s_even, t_odd, s_odd = exps
+
+    def work(i, carry):
+        even_max, odd_inv = carry
+        matmuls(i)
+        odd_max = tops(2 * i + 1)
+        score_grads(jnp.maximum(2 * i - 1, 0), *odd_inv, t_odd, s_odd)
+        even_inv = sums(2 * i, *even_max, t_even, s_even)
+        next_max = tops(jnp.minimum(2 * i + 2, groups - 1))
+        score_grads(2 * i, *even_inv, t_even, s_even)
+        odd_inv = sums(2 * i + 1, *odd_max, t_odd, s_odd)
+        return next_max, odd_inv
+
+    zero = jnp.zeros((group, LANES), jnp.float32)
+    _, odd_inv = lax.fori_loop(0, pieces, work, (tops(0), (zero, zero)))
+    score_grads(groups - 1, *odd_inv, t_odd, s_odd)
+
+
+def relation_body(t_keys, s_keys, s_turned, kl_out, grad_out,
+                  t_a, s_a, g_a, t_b, s_b, g_b, t_even, s_even, t_odd, s_odd, row_acc, key_acc, *, steps, group, t_scale, s_scale):
+    step = pl.program_id(0)
+    block = t_a.shape[0]
+    keys = t_a.shape[1]
+    last = pl.num_programs(0) - 3
+    score_row = jnp.minimum(step, last) % steps * block
+    grad_row = jnp.maximum(step - 2, 0) % steps * block
+
+    @pl.when(jnp.logical_or(step < 2, (step - 2) % steps == 0))
     def _():
+        row_acc[...] = jnp.zeros_like(row_acc)
         key_acc[...] = jnp.zeros_like(key_acc)
 
-    row_acc[pl.ds(pl.multiple_of(step * block, block), block), :] = jnp.dot(
-        g_buf[...], s_keys[...], preferred_element_type=jnp.float32
-    )
-    for c in range(keys // chunk):
-        at = slice(c * chunk, (c + 1) * chunk)
-        key_acc[:, at] += jnp.dot(s_rows_t[...], g_buf[:, at], preferred_element_type=jnp.float32)
-
-    @pl.when(step == pl.num_programs(0) - 1)
+    for parity, (t_new, s_new, g_new, t_old, s_old, g_old) in enumerate(
+        ((t_a, s_a, g_a, t_b, s_b, g_b), (t_b, s_b, g_b, t_a, s_a, g_a))
+    ):
+        @pl.when(step % 2 == parity)
+        def _():
+            stage(t_keys, s_keys, s_turned, kl_out, t_new, s_new, t_old, s_old, g_new, g_old,
+                  (t_even, s_even, t_odd, s_odd), row_acc, key_acc,
+                  score_row=score_row, grad_row=grad_row, group=group, t_scale=t_scale, s_scale=s_scale)
+
+    @pl.when(jnp.logical_and(step >= 2, (step - 2) % steps == steps - 1))
     def _():
         def finish(c, carry):
             at = pl.ds(pl.multiple_of(c * LANES, LANES), LANES)
-            grad_out[at, :] = ((row_acc[at, :] + key_acc[:, at].T) * s_scale).astype(jnp.bfloat16)
+            grad_out[at, :] = ((row_acc[:, at] + key_acc[:, at]).T * s_scale).astype(jnp.bfloat16)
             return carry
-
         lax.fori_loop(0, keys // LANES, finish, 0)
 
 
-def relation(teacher, student, part, parts):
+def relation(teacher, student, parts):
     keys = teacher.shape[0]
     t_width = teacher.shape[1] // parts
     s_width = student.shape[1] // parts
     block = min(256, keys)
-    group = 16
-    chunk = min(1024, keys)
+    group = 32
     steps = keys // block
+    last = parts * steps - 1
+    score_part = lambda i: jnp.minimum(i, last) // steps
+    grad_part = lambda i: jnp.maximum(i - 2, 0) // steps
     kl, grad = pl.pallas_call(
-        functools.partial(
-            relation_body, group=group, chunk=chunk, t_scale=t_width ** (-0.5), s_scale=s_width ** (-0.5)
-        ),
-        grid=(steps,),
+        functools.partial(relation_body, steps=steps, group=group, t_scale=t_width ** (-0.5), s_scale=s_width ** (-0.5)),
+        grid=(parts * steps + 2,),
         in_specs=[
-            pl.BlockSpec((block, t_width), lambda i: (i, part)),
-            pl.BlockSpec((keys, t_width), lambda i: (0, part)),
-            pl.BlockSpec((block, s_width), lambda i: (i, part)),
-            pl.BlockSpec((keys, s_width), lambda i: (0, part)),
-            pl.BlockSpec((s_width, block), lambda i: (part, i)),
+            pl.BlockSpec((keys, t_width), lambda i: (0, score_part(i))),
+            pl.BlockSpec((keys, s_width), lambda i: (0, score_part(i))),
+            pl.BlockSpec((s_width, keys), lambda i: (grad_part(i), 0)),
         ],
         out_specs=[
-            pl.BlockSpec((1, block, LANES), lambda i: (i, 0, 0)),
-            pl.BlockSpec((keys, s_width), lambda i: (0, 0)),
+            pl.BlockSpec((1, block, LANES), lambda i: (jnp.clip(i - 1, 0, last), 0, 0)),
+            pl.BlockSpec((keys, s_width), lambda i: (0, grad_part(i))),
         ],
         out_shape=[
-            jax.ShapeDtypeStruct((steps, block, LANES), jnp.float32),
-            jax.ShapeDtypeStruct((keys, s_width), jnp.bfloat16),
+            jax.ShapeDtypeStruct((parts * steps, block, LANES), jnp.float32),
+            jax.ShapeDtypeStruct(student.shape, jnp.bfloat16),
         ],
         scratch_shapes=[
             pltpu.VMEM((block, keys), jnp.float32),
             pltpu.VMEM((block, keys), jnp.float32),
             pltpu.VMEM((block, keys), jnp.bfloat16),
-            pltpu.VMEM((keys, s_width), jnp.float32),
+        ] * 2 + [pltpu.VMEM((group, keys), jnp.float32)] * 4 + [
+            pltpu.VMEM((s_width, keys), jnp.float32),
             pltpu.VMEM((s_width, keys), jnp.float32),
         ],
         compiler_params=pltpu.CompilerParams(
-            dimension_semantics=("arbitrary",), vmem_limit_bytes=40 * 1024 * 1024
+            dimension_semantics=("arbitrary",), vmem_limit_bytes=60 * 1024 * 1024
         ),
         name="relation",
-    )(teacher, teacher, student, student, student.T)
-    return kl[:, :, 0].reshape(keys), grad
+    )(teacher, student, student.T)
+    return kl[:, :, 0].reshape(parts, keys), grad
+
+
+MESH = pl.DeviceIdType.MESH
+
+
+def gather_body(
+    teacher, hidden, weight, teacher_out, student_out, hidden_out,
+    h_full, w_full, total, s_loc, t_stage, h_send, h_recv, w_up, w_down, w_side, w_recv, w_side_recv,
+    t_send, t_recv, s_send, s_recv, local_sem,
+    *, line, pairs, members, tps,
+):
+    dp = lax.axis_index("dp")
+    tp = lax.axis_index("tp")
+    z, x = dp // pairs, dp % pairs
+    size = line * pairs
+    base = dp // members * members
+    spot = dp % members
+    token_rows = hidden.shape[0]
+    feats = hidden.shape[1]
+    depth = weight.shape[0]
+    width = weight.shape[1]
+
+    barrier = pltpu.get_barrier_semaphore()
+    for k in range(1, size):
+        pl.semaphore_signal(barrier, inc=1, device_id={"dp": (dp + k) % size}, device_id_type=MESH)
+    for k in range(1, tps):
+        pl.semaphore_signal(barrier, inc=1, device_id={"tp": (tp + k) % tps}, device_id_type=MESH)
+    pl.semaphore_wait(barrier, size - 1 + tps - 1)
+
+    half = tp // 2
+    core = tp % 2
+    mate = half * 2 + 1 - core
+    across = (1 - half) * 2 + core
+    side = z * pairs + 1 - x
+
+    def feat_cols(owner):
+        return pl.ds(pl.multiple_of(owner * feats, feats), feats)
+
+    def weight_rows(zo, xo):
+        return pl.ds(pl.multiple_of((zo * pairs + xo) * depth, depth), depth)
+
+    def remote(src, dst, send, recv, where):
+        return pltpu.make_async_remote_copy(
+            src_ref=src, dst_ref=dst, send_sem=send, recv_sem=recv, device_id=where, device_id_type=MESH
+        )
+
+    def hidden_copy(n, src, owner, where):
+        return remote(src, h_full.at[:, feat_cols(owner)], h_send.at[n], h_recv.at[n], where)
+
+    def weight_copy(src, zo, sems, where):
+        return remote(src, w_full.at[weight_rows(zo, x), :], sems.at[zo], w_recv.at[zo], where)
+
+    def weight_aside(src, zo, xo):
+        return remote(src, w_full.at[weight_rows(zo, xo), :], w_side.at[zo], w_side_recv.at[zo], {"dp": side})
+
+    def onward(src, zo, up, down):
+        if up:
+            @pl.when(z < line - 1)
+            def _():
+                weight_copy(src, zo, w_up, {"dp": dp + pairs}).start()
+        if down:
+            @pl.when(z > 0)
+            def _():
+                weight_copy(src, zo, w_down, {"dp": dp - pairs}).start()
+        weight_aside(src, zo, x).start()
+
+    hidden_copy(0, hidden, tp, {"tp": across}).start()
+    hidden_copy(1, hidden, tp, {"tp": mate}).start()
+    onward(weight, z, True, True)
+    h_own = pltpu.make_async_copy(hidden, h_full.at[:, feat_cols(tp)], local_sem.at[0])
+    h_own.start()
+    w_own = pltpu.make_async_copy(weight, w_full.at[weight_rows(z, x), :], local_sem.at[1])
+    w_own.start()
+    t_cols = teacher.shape[1] // members
+    s_cols = width // members
+
+    def part(k, n):
+        return pl.ds(pl.multiple_of(k * n, n), n)
+
+    own_rows = part(spot, token_rows)
+    t_in = pltpu.make_async_copy(teacher.at[:, part(spot, t_cols)], t_stage, local_sem.at[2])
+    t_in.start()
+
+    def step(d, below):
+        zo = z - d if below else z + d
+        there = zo >= 0 if below else zo < line
+        return zo, there
+
+    def arrive(d):
+        for below in (True, False):
+            zo, there = step(d, below)
+
+            @pl.when(there)
+            def _():
+                weight_copy(w_full.at[weight_rows(zo, x), :], zo, w_up, {"dp": dp}).wait_recv()
+                onward(w_full.at[weight_rows(zo, x), :], zo, below, not below)
+
+    def add(zo, xo, first=False):
+        rows = 256 if token_rows % 256 == 0 else token_rows
+        cols = 256 if width % 256 == 0 else width
+        span = weight_rows(zo, xo)
+
+        def tile(i, carry):
+            at = part(i // (width // cols), rows)
+            to = part(i % (width // cols), cols)
+            term = jnp.dot(h_full[at, span], w_full[span, to], preferred_element_type=jnp.float32)
+            total[at, to] = term if first else total[at, to] + term
+            return carry
+
+        lax.fori_loop(0, (token_rows // rows) * (width // cols), tile, 0)
+
+    def add_mine(d):
+        for below in (True, False):
+            zo, there = step(d, below)
+
+            @pl.when(there)
+            def _():
+                add(zo, x)
+
+    def add_side(d):
+        for below in (True, False) if d else (True,):
+            zo, there = step(d, below)
+
+            @pl.when(there)
+            def _():
+                weight_aside(w_full.at[weight_rows(zo, 1 - x), :], zo, 1 - x).wait_recv()
+                add(zo, 1 - x)
+
+    arrive(1)
+    hidden_copy(0, hidden, across, {"tp": across}).wait_recv()
+    hidden_copy(2, h_full.at[:, feat_cols(across)], across, {"tp": mate}).start()
+    hidden_copy(1, hidden, mate, {"tp": mate}).wait_recv()
+    h_own.wait()
+    w_own.wait()
+    far = (1 - half) * 2 + 1 - core
+    hidden_copy(2, hidden, far, {"tp": mate}).wait_recv()
+    h_out = pltpu.make_async_copy(h_full, hidden_out, local_sem.at[0])
+    h_out.start()
+    add(z, x, True)
+    add_side(0)
+    add_mine(1)
+    for d in range(2, line):
+        arrive(d)
+        if d == line - 1:
+            for k in range(1, members):
+                to = (spot + k) % members
+                remote(
+                    teacher.at[:, part(to, t_cols)], teacher_out.at[own_rows, :], t_send.at[k], t_recv.at[k], {"dp": base + to}
+                ).start()
+        add_side(d - 1)
+        add_mine(d)
+    add_side(line - 1)
+
+    s_loc[...] = total[...].astype(jnp.bfloat16)
+    for k in range(1, members):
+        to = (spot + k) % members
+        remote(
+            s_loc.at[:, part(to, s_cols)], student_out.at[own_rows, :], s_send.at[k], s_recv.at[k], {"dp": base + to}
+        ).start()
+    t_in.wait()
+    t_out = pltpu.make_async_copy(t_stage, teacher_out.at[own_rows, :], local_sem.at[2])
+    t_out.start()
+    s_own = pltpu.make_async_copy(s_loc.at[:, part(spot, s_cols)], student_out.at[own_rows, :], local_sem.at[1])
+    s_own.start()
+
+    hidden_copy(0, hidden, tp, {"tp": across}).wait_send()
+    hidden_copy(1, hidden, tp, {"tp": mate}).wait_send()
+    hidden_copy(2, hidden, across, {"tp": mate}).wait_send()
+    for d in range(line):
+        for below in (True, False) if d else (True,):
+            zo, there = step(d, below)
+
+            @pl.when(jnp.logical_and(there, z < line - 1) if below else False)
+            def _():
+                weight_copy(weight, zo, w_up, {"dp": dp}).wait_send()
+
+            @pl.when(jnp.logical_and(there, z > 0) if not below or d == 0 else False)
+            def _():
+                weight_copy(weight, zo, w_down, {"dp": dp}).wait_send()
+
+            @pl.when(there)
+            def _():
+                weight_aside(weight, zo, x).wait_send()
+    for k in range(1, members):
+        source = (spot + members - k) % members
+        from_rows = part(source, token_rows)
+        t_copy = remote(
+            teacher.at[:, part(spot, t_cols)], teacher_out.at[from_rows, :], t_send.at[k], t_recv.at[k], {"dp": base + source}
+        )
+        s_copy = remote(
+            s_loc.at[:, part(spot, s_cols)], student_out.at[from_rows, :], s_send.at[k], s_recv.at[k], {"dp": base + source}
+        )
+        t_copy.wait()
+        s_copy.wait()
+    h_out.wait()
+    t_out.wait()
+    s_own.wait()
+
+
+def gather_and_project(teacher_query, student_hidden, query_weight):
+    tps, size = lax.axis_size("tp"), lax.axis_size("dp")
+    members = size // NSEQ
+    pairs = 2
+    line = size // pairs
+    rows, feats = student_hidden.shape
+    depth, width = query_weight.shape
+    dma = pltpu.SemaphoreType.DMA
+    any_space = pl.BlockSpec(memory_space=pl.ANY)
+    return pl.pallas_call(
+        functools.partial(gather_body, line=line, pairs=pairs, members=members, tps=tps),
+        in_specs=[any_space] * 3,
+        out_specs=[any_space] * 3,
+        out_shape=[
+            jax.ShapeDtypeStruct((members * rows, teacher_query.shape[1] // members), jnp.bfloat16),
+            jax.ShapeDtypeStruct((members * rows, width // members), jnp.bfloat16),
+            jax.ShapeDtypeStruct((rows, tps * feats), jnp.bfloat16),
+        ],
+        scratch_shapes=[
+            pltpu.VMEM((rows, tps * feats), jnp.bfloat16),
+            pltpu.VMEM((size * depth, width), jnp.bfloat16),
+            pltpu.VMEM((rows, width), jnp.float32),
+            pltpu.VMEM((rows, width), jnp.bfloat16),
+            pltpu.VMEM((rows, teacher_query.shape[1] // members), jnp.bfloat16),
+            dma((3,)), dma((3,)), dma((line,)), dma((line,)), dma((line,)), dma((line,)), dma((line,)),
+            dma((members,)), dma((members,)), dma((members,)), dma((members,)), dma((3,)),
+        ],
+        compiler_params=pltpu.CompilerParams(
+            collective_id=0, has_side_effects=True, vmem_limit_bytes=60 * 1024 * 1024
+        ),
+        name="gather_and_project",
+    )(teacher_query, student_hidden, query_weight)
 
 
 def heads_of_one_sequence(teacher_query, student_hidden, query_weight):
     members = lax.axis_size("dp") // NSEQ
     mine = RHEADS // lax.axis_size("tp") // members
     groups = [[s * members + k for k in range(members)] for s in range(NSEQ)]
-    to_heads = functools.partial(
-        lax.all_to_all, axis_name="dp", split_axis=1, concat_axis=0, axis_index_groups=groups, tiled=True
-    )
-    teacher_all = to_heads(teacher_query)
-    hidden_full = lax.all_gather(student_hidden, "tp", axis=1, tiled=True)
-    weight_full = lax.all_gather(query_weight, "dp", axis=0, tiled=True)
-    student_query = jnp.dot(hidden_full, weight_full, preferred_element_type=jnp.float32).astype(jnp.bfloat16)
-    student_all = to_heads(student_query)
+    teacher_all, student_all, hidden_full = gather_and_project(teacher_query, student_hidden, query_weight)
     rows_of = [0.0] * NSEQ
-    grads = []
+    kl, grad = relation(teacher_all, student_all, mine)
     for m in range(mine):
-        kl, grad = relation(teacher_all, student_all, m, mine)
         for s in range(NSEQ):
             pairs = [(s * members + k, k * mine + m) for k in range(members)]
-            rows_of[s] = rows_of[s] + lax.ppermute(kl, "dp", pairs)
-        part = lax.all_to_all(
-            grad, "dp", split_axis=0, concat_axis=1, axis_index_groups=groups, tiled=True
-        )
-        grads.append(part.reshape(part.shape[0], members, 1, part.shape[1] // members))
-    grad_rows = jnp.concatenate(grads, axis=2).reshape(student_query.shape)
+            rows_of[s] = rows_of[s] + lax.ppermute(kl[m], "dp", pairs)
+    grad_rows = lax.all_to_all(
+        grad, "dp", split_axis=0, concat_axis=1, axis_index_groups=groups, tiled=True
+    )
     partial = lax.dot_general(
         hidden_full, grad_rows, (((0,), (0,)), ((), ())), preferred_element_type=jnp.float32
     )

time: 795 us -> 634 us (0.80)
  waiting for transfers between devices: 424 us -> 185 us
  Pallas kernels: 250 us -> 381 us
  blocking collectives: 16.6 us -> 0 us
  matrix products: 28.9 us -> 14.6 us
  between operations: 14.2 us -> 0.75 us
    all_gather x2 -> x0, waiting for transfers between devices: 189 us -> none  [the longest x1 127 us: heads_of_one_sequence(): weight_full = lax.all_gather(query_weight, 'dp', axis=0, tiled=True)]
    pallas_call x2, Pallas kernels: 250 us -> 381 us  [the longest x1 195 us: relation(): pl.pallas_call(functools.partial(relation_body, steps=steps, group=group,...]
    all_to_all x2 -> x0, waiting for transfers between devices: 62.5 us -> none  [the longest x1 42.6 us: heads_of_one_sequence(): teacher_all = to_heads(teacher_query)]
    all_to_all x1 -> x0, blocking collectives: 16.6 us -> none  [heads_of_one_sequence(): lax.all_to_all(grad, 'dp', split_axis=0, concat_axis=1, axis_index_groups...]
    dot_general x1 -> x0, matrix products: 14.7 us -> none  [heads_of_one_sequence(): jnp.dot(hidden_full, weight_full, preferred_element_type=jnp.float32)]
    all_to_all x1, waiting for transfers between devices: 0.01 us -> 13.9 us  [heads_of_one_sequence(): lax.all_to_all(grad, 'dp', split_axis=0, concat_axis=1, axis_index_groups...]
    dot_general x0 -> x1, local copies, waits for them, and re-layouts: none -> 12 us  [heads_of_one_sequence(): lax.dot_general(hidden_full, grad_rows, (((0,), (0,)), ((), ())), preferr...]
    all_to_all x3 -> x0, local copies, waits for them, and re-layouts: 9.35 us -> none  [the longest x2 4.83 us: heads_of_one_sequence(): student_all = to_heads(student_query)]
  transfers between devices with their start and end apart: 10 -> 6, of which waited for: 6 -> 2; matrix products, arithmetic and copies ran while one was open for 2% -> 3% of each run, Pallas kernels for 16% -> 0%
where the time goes in v2:
time: 634 us; the launch traced here: 633 us
  Pallas kernels  381 us (60%)
  waiting for transfers between devices  185 us (29%)
  local copies, waits for them, and re-layouts  25.6 us (4%)
  starting transfers between devices  17.9 us (3%)
  matrix products  14.6 us (2%)
  other arithmetic  7.54 us (1%)
    pallas_call x1, Pallas kernels, relation(): pl.pallas_call(functools.partial(relation_body, steps=steps, group=group,...  195 us
    pallas_call x1, Pallas kernels, gather_and_project(): pl.pallas_call(functools.partial(gather_body, line=line, pairs=pairs, mem...  186 us
    ppermute x4, waiting for transfers between devices, heads_of_one_sequence(): rows_of[s] = rows_of[s] + lax.ppermute(kl[m], 'dp', pairs)  171 us
    dot_general x1, matrix products, heads_of_one_sequence(): lax.dot_general(hidden_full, grad_rows, (((0,), (0,)), ((), ())), preferr...  14.6 us
    all_to_all x1, waiting for transfers between devices, heads_of_one_sequence(): lax.all_to_all(grad, 'dp', split_axis=0, concat_axis=1, axis_index_groups...  13.9 us
  transfers between devices with their start and end apart: 6, of which 2 were waited for; matrix products, arithmetic and copies ran while one was open for 3% of the time, Pallas kernels for 0%

profile of v2, /device:TPU:0, one launch (start us, length us, event | category | flops | bytes accessed | tf_op | source)
XLA Modules:
  0.0 632.7 jit_solution(16504688010458528857)
XLA Ops:
  0.6 186.3 %gather_and_project.1 = (bf16[4096,512]{1,0:T(8,128)(2,1)}, bf16[4096,256]{1,0:T(8,128)(2,1)}, bf16[1024,4096]{1,0:T(8,128)(2,1)}) custom-call(bf16[1024,2048]{1,0:T(8,128)(2,1)} %teacher.1, bf16[1024,1024]{1,0:T(8,128)(2,1)} %hidden.1, bf16[512,1024]{1,0:T(8,128)(2,1)} %weight.1), custom_call_target="tpu_custom_call" | custom-call | tf_op jit(solution)/shard_map/gather_and_project/pallas_call | solution.py:399
  186.9 4.1 copy.8
  191.0 194.6 %relation.1 = (f32[32,256,128]{2,1,0:T(8,128)}, bf16[4096,256]{1,0:T(8,128)(2,1)}) custom-call(bf16[4096,512]{1,0:T(8,128)(2,1)} %get-tuple-element.7.t_keys, bf16[4096,256]{1,0:T(8,128)(2,1)} %get-tuple-element.8.s_keys, bf16[256,4096]{1,0:T(8,128)(2,1)} %bitcast.15), custom_call_target="tpu_custom_call" | custom-call | tf_op jit(solution)/shard_map/relation/pallas_call | solution.py:161
  385.6 3.8 all-to-all-start
  389.4 12.0 %copy.11 = bf16[4096,1024]{1,0:T(8,128)(2,1)} copy(bf16[4096,1024]{0,1:T(8,128)(2,1)} %bitcast.12) | data formatting | bytes 16777216 | tf_op jit(solution)/shard_map/dot_general | solution.py:438
  401.4 13.9 %all-to-all-done = bf16[4,1024,256]{2,1,0:T(8,128)(2,1)S(1)} async-done(((bf16[4,1024,256]{2,1,0:T(8,128)(2,1)}), bf16[4,1024,256]{2,1,0:T(8,128)(2,1)S(1)}, u32[]{:S(2)}, u32[]{:S(2)}) %all-to-all-start) | async-done | bytes 2097184 | tf_op jit(solution)/shard_map/all_to_all | solution.py:435
  415.3 2.9 copy.9
  418.2 3.2 reshape.17
  421.5 14.6 %convolution_convert_fusion = bf16[8,512,1024]{2,1,0:T(8,128)(2,1)} fusion(bf16[8,512,1024]{2,1,0:T(8,128)(2,1)} %bitcast.13, bf16[1024,1024,1]{1,0,2:T(8,128)(2,1)S(1)} %reshape.17), kind=kOutput, calls=%fused_computation.1 | convolution fusion | flops 8594128896 | bytes 18874368 | tf_op jit(solution)/shard_map/dot_general | solution.py:438
  436.1 5.0 all-to-all-start.1
  441.1 3.4 slice_reduce_fusion
  444.5 1.3 collective-permute-start.2
  445.8 0.7 collective-permute-start.3
  446.5 0.7 collective-permute-start
  447.2 6.5 %collective-permute-start.1 = (f32[4096]{0:T(1024)S(1)}, f32[4096]{0:T(1024)S(1)}, u32[]{:S(2)}, u32[]{:S(2)}) collective-permute-start(f32[4096]{0:T(1024)S(1)} %bitcast.23), channel_id=1, source_target_pairs={{0,1},{1,3},{2,5},{3,7},{8,9},{9,11},{10,13},{11,15},{16,17},{17,1... | collective-permute-start | bytes 49160 | tf_op jit(solution)/shard_map/ppermute | solution.py:434
  453.7 171.5 %collective-permute-done.2 = f32[4096]{0:T(1024)S(1)} collective-permute-done((f32[4096]{0:T(1024)S(1)}, f32[4096]{0:T(1024)S(1)}, u32[]{:S(2)}, u32[]{:S(2)}) %collective-permute-start.2) | collective-permute-done | bytes 16416 | tf_op jit(solution)/shard_map/ppermute | solution.py:434
  625.1 0.0 collective-permute-done.3
  625.2 0.0 collective-permute-done
  625.2 0.0 collective-permute-done.1
  625.2 0.6 pad_maximum_fusion
  625.8 0.0 all-to-all-done.1
  625.8 6.9 %convert_reduce_fusion = f32[512,1024]{1,0:T(8,128)} fusion(bf16[8,512,1024]{2,1,0:T(8,128)(2,1)} %all-to-all-done.1), kind=kLoop, calls=%fused_computation | loop fusion | flops 7864320 | bytes 10485760 | tf_op jit(solution)/shard_map/reduce_sum | solution.py:444
  (4 shorter events, 0.0 us)
Async XLA Ops:
  385.6 29.7 %all-to-all-start = ((bf16[4,1024,256]{2,1,0:T(8,128)(2,1)}), bf16[4,1024,256]{2,1,0:T(8,128)(2,1)S(1)}, u32[]{:S(2)}, u32[]{:S(2)}) async-start(bf16[4,1024,256]{2,1,0:T(8,128)(2,1)} %bitcast.16), calls=%async_computation | async-start | bytes 4194304 | tf_op jit(solution)/shard_map/all_to_all | solution.py:435
  436.1 189.7 %all-to-all-start.1 = ((bf16[8,512,1024]{2,1,0:T(8,128)(2,1)}), bf16[8,512,1024]{2,1,0:T(8,128)(2,1)}, u32[]{:S(2)}, u32[]{:S(2)}) async-start(bf16[8,512,1024]{2,1,0:T(8,128)(2,1)} %convolution_convert_fusion), calls=%async_computation.1 | async-start | bytes 16777216 | tf_op jit(solution)/shard_map/all_to_all | solution.py:443
  444.5 180.6 %collective-permute-start.2 = (f32[4096]{0:T(1024)S(1)}, f32[4096]{0:T(1024)S(1)}, u32[]{:S(2)}, u32[]{:S(2)}) collective-permute-start(f32[4096]{0:T(1024)S(1)} %bitcast.20), channel_id=1, source_target_pairs={{4,0},{5,2},{6,4},{7,6},{12,8},{13,10},{14,12},{15,14},{20,16},{21... | collective-permute-start | bytes 49160 | tf_op jit(solution)/shard_map/ppermute | solution.py:434
  445.8 179.3 %collective-permute-start.3 = (f32[4096]{0:T(1024)S(1)}, f32[4096]{0:T(1024)S(1)}, u32[]{:S(2)}, u32[]{:S(2)}) collective-permute-start(f32[4096]{0:T(1024)S(1)} %bitcast.22), channel_id=1, source_target_pairs={{4,1},{5,3},{6,5},{7,7},{12,9},{13,11},{14,13},{15,15},{20,17},{21... | collective-permute-start | bytes 49160 | tf_op jit(solution)/shard_map/ppermute | solution.py:434
  446.5 178.7 %collective-permute-start = (f32[4096]{0:T(1024)S(1)}, f32[4096]{0:T(1024)S(1)}, u32[]{:S(2)}, u32[]{:S(2)}) collective-permute-start(f32[4096]{0:T(1024)S(1)} %bitcast.21), channel_id=1, source_target_pairs={{0,0},{1,2},{2,4},{3,6},{8,8},{9,10},{10,12},{11,14},{16,16},{17,1... | collective-permute-start | bytes 49160 | tf_op jit(solution)/shard_map/ppermute | solution.py:434
  447.2 178.0 %collective-permute-start.1 = (f32[4096]{0:T(1024)S(1)}, f32[4096]{0:T(1024)S(1)}, u32[]{:S(2)}, u32[]{:S(2)}) collective-permute-start(f32[4096]{0:T(1024)S(1)} %bitcast.23), channel_id=1, source_target_pairs={{0,1},{1,3},{2,5},{3,7},{8,9},{9,11},{10,13},{11,15},{16,17},{17,1... | collective-permute-start | bytes 49160 | tf_op jit(solution)/shard_map/ppermute | solution.py:434

commit v3 on v2

--- a/solution.py
+++ b/solution.py
@@ -421,6 +421,130 @@
     )(teacher_query, student_hidden, query_weight)
 
 
+def reduce_body(
+    hidden, grad, out, h_all, g_all, own, x_out, x_in, z_out, z_in,
+    g_send, g_recv, x_send, x_recv, z_send, z_recv, local_sem,
+    *, line, pairs, members,
+):
+    dp = lax.axis_index("dp")
+    z, x = dp // pairs, dp % pairs
+    size = line * pairs
+    base = dp // members * members
+    spot = dp % members
+    token_rows = h_all.shape[0]
+    depth = out.shape[0]
+    g_cols = grad.shape[1]
+    tall = 256 if depth % 256 == 0 else depth
+
+    barrier = pltpu.get_barrier_semaphore()
+    for k in range(1, size):
+        pl.semaphore_signal(barrier, inc=1, device_id={"dp": (dp + k) % size}, device_id_type=MESH)
+    h_in = pltpu.make_async_copy(hidden, h_all, local_sem.at[0])
+    h_in.start()
+    pl.semaphore_wait(barrier, size - 1)
+
+    def part(k, n):
+        return pl.ds(pl.multiple_of(k * n, n), n)
+
+    def remote(src, dst, send, recv, to):
+        return pltpu.make_async_remote_copy(
+            src_ref=src, dst_ref=dst, send_sem=send, recv_sem=recv, device_id={"dp": to}, device_id_type=MESH
+        )
+
+    def grad_copy(k, to):
+        return remote(
+            grad.at[part(to % members, token_rows), :], g_all.at[:, part(spot, g_cols)], g_send.at[k], g_recv.at[k], to
+        )
+
+    for k in range(1, members):
+        grad_copy(k, base + (spot + k) % members).start()
+    g_own = pltpu.make_async_copy(
+        grad.at[part(spot, token_rows), :], g_all.at[:, part(spot, g_cols)], local_sem.at[1]
+    )
+    g_own.start()
+    h_in.wait()
+    g_own.wait()
+    for k in range(1, members):
+        grad_copy(k, base + (spot + members - k) % members).wait_recv()
+
+    shifts = [line // 2] + [s for s in range(line - 1, 0, -1) if s != line // 2] + [0]
+
+    def multiply(zo, xo, into):
+        def tile(i, carry):
+            at = pl.ds(pl.multiple_of((zo * pairs + xo) * depth + i * tall, tall), tall)
+            term = lax.dot_general(
+                h_all[:, at], g_all[...], (((0,), (0,)), ((), ())), preferred_element_type=jnp.float32
+            )
+            into[part(i, tall), :] = term.astype(into.dtype)
+            return carry
+
+        lax.fori_loop(0, depth // tall, tile, 0)
+
+    def aside(n):
+        return remote(x_out.at[n], x_in.at[n], x_send.at[n], x_recv.at[n], z * pairs + 1 - x)
+
+    def along(s, zo):
+        return remote(z_out.at[s], z_in.at[s], z_send.at[s], z_recv.at[s], zo * pairs + x)
+
+    for n, s in enumerate(shifts):
+        multiply((z + s) % line, 1 - x, x_out.at[n])
+        aside(n).start()
+    for n, s in enumerate(shifts):
+        multiply((z + s) % line, x, own.at[n])
+    for n, s in enumerate(shifts):
+        aside(n).wait_recv()
+        if s:
+            z_out[s] = (own[n] + x_in[n].astype(jnp.float32)).astype(jnp.bfloat16)
+            along(s, (z + s) % line).start()
+        else:
+            own[n] = own[n] + x_in[n].astype(jnp.float32)
+    for s in shifts[:-1]:
+        along(s, (z + s) % line).wait_recv()
+    total = own[line - 1]
+    for s in shifts[:-1]:
+        total = total + z_in[s].astype(jnp.float32)
+    out[...] = total
+
+    for k in range(1, members):
+        grad_copy(k, base + (spot + k) % members).wait_send()
+    for n, s in enumerate(shifts):
+        aside(n).wait_send()
+        if s:
+            along(s, (z + s) % line).wait_send()
+
+
+def reduce_weight(hidden_full, grad):
+    size = lax.axis_size("dp")
+    members = size // NSEQ
+    pairs = 2
+    line = size // pairs
+    rows, feats = hidden_full.shape
+    width = grad.shape[1] * members
+    depth = feats // size
+    dma = pltpu.SemaphoreType.DMA
+    any_space = pl.BlockSpec(memory_space=pl.ANY)
+    return pl.pallas_call(
+        functools.partial(reduce_body, line=line, pairs=pairs, members=members),
+        in_specs=[any_space] * 2,
+        out_specs=pl.BlockSpec(memory_space=pltpu.VMEM),
+        out_shape=jax.ShapeDtypeStruct((depth, width), jnp.float32),
+        scratch_shapes=[
+            pltpu.VMEM((rows, feats), jnp.bfloat16),
+            pltpu.VMEM((rows, width), jnp.bfloat16),
+            pltpu.VMEM((line, depth, width), jnp.float32),
+            pltpu.VMEM((line, depth, width), jnp.bfloat16),
+            pltpu.VMEM((line, depth, width), jnp.bfloat16),
+            pltpu.VMEM((line, depth, width), jnp.bfloat16),
+            pltpu.VMEM((line, depth, width), jnp.bfloat16),
+            dma((members,)), dma((members,)), dma((line,)), dma((line,)), dma((line,)), dma((line,)), dma((2,)),
+        ],
+        compiler_params=pltpu.CompilerParams(
+            collective_id=1, has_side_effects=True, vmem_limit_bytes=60 * 1024 * 1024
+        ),
+        name="reduce_weight",
+    )(hidden_full, grad)
+
+
 def heads_of_one_sequence(teacher_query, student_hidden, query_weight):
     members = lax.axis_size("dp") // NSEQ
     mine = RHEADS // lax.axis_size("tp") // members
@@ -432,16 +556,8 @@
         for s in range(NSEQ):
             pairs = [(s * members + k, k * mine + m) for k in range(members)]
             rows_of[s] = rows_of[s] + lax.ppermute(kl[m], "dp", pairs)
-    grad_rows = lax.all_to_all(
-        grad, "dp", split_axis=0, concat_axis=1, axis_index_groups=groups, tiled=True
-    )
-    partial = lax.dot_general(
-        hidden_full, grad_rows, (((0,), (0,)), ((), ())), preferred_element_type=jnp.float32
-    )
-    size = lax.axis_size("dp")
-    pieces = partial.reshape(size, partial.shape[0] // size, partial.shape[1]).astype(jnp.bfloat16)
-    landed = lax.all_to_all(pieces, "dp", split_axis=0, concat_axis=0, tiled=True)
-    return jnp.concatenate(rows_of).reshape(1, NSEQ * SEQ), jnp.sum(landed.astype(jnp.float32), axis=0)
+    weight_grad = reduce_weight(hidden_full, grad)
+    return jnp.concatenate(rows_of).reshape(1, NSEQ * SEQ), weight_grad
 
 
 def local(teacher_query, student_hidden, query_weight):

time: 634 us -> 547 us (0.86)
  waiting for transfers between devices: 185 us -> 0.01 us
  Pallas kernels: 381 us -> 528 us
  local copies, waits for them, and re-layouts: 25.6 us -> 10.6 us
  matrix products: 14.6 us -> 0 us
  starting transfers between devices: 17.9 us -> 6.96 us
  other arithmetic: 7.54 us -> 0.63 us
    ppermute x4, waiting for transfers between devices: 171 us -> 0.01 us  [heads_of_one_sequence(): rows_of[s] = rows_of[s] + lax.ppermute(kl[m], 'dp', pairs)]
    pallas_call x0 -> x1, Pallas kernels: none -> 147 us  [reduce_weight(): pl.pallas_call(functools.partial(reduce_body, line=line, pairs=pairs, mem...]
    dot_general x1 -> x0, matrix products: 14.6 us -> none  [heads_of_one_sequence(): lax.dot_general(hidden_full, grad_rows, (((0,), (0,)), ((), ())), preferr...]
    all_to_all x2 -> x0, waiting for transfers between devices: 13.9 us -> none  [the longest x1 13.9 us: heads_of_one_sequence(): lax.all_to_all(grad, 'dp', split_axis=0, concat_axis=1, axis_index_groups...]
    dot_general x1 -> x0, local copies, waits for them, and re-layouts: 12 us -> none  [heads_of_one_sequence(): lax.dot_general(hidden_full, grad_rows, (((0,), (0,)), ((), ())), preferr...]
    all_to_all x2 -> x0, starting transfers between devices: 8.81 us -> none  [the longest x1 5.02 us: heads_of_one_sequence(): lax.all_to_all(pieces, 'dp', split_axis=0, concat_axis=0, tiled=True)]
    reduce_sum x1 -> x0, other arithmetic: 6.91 us -> none  [heads_of_one_sequence(): jnp.sum(landed.astype(jnp.float32), axis=0)]
  transfers between devices with their start and end apart: 6 -> 4, of which waited for: 2 -> 0; matrix products, arithmetic and copies ran while one was open for 3% -> 0% of each run, Pallas kernels for 0% -> 27%
where the time goes in v3:
time: 547 us
  Pallas kernels  528 us (97%)
  local copies, waits for them, and re-layouts  10.6 us (2%)
  starting transfers between devices  6.96 us (1%)
    pallas_call x1, Pallas kernels, relation(): pl.pallas_call(functools.partial(relation_body, steps=steps, group=group,...  195 us
    pallas_call x1, Pallas kernels, gather_and_project(): pl.pallas_call(functools.partial(gather_body, line=line, pairs=pairs, mem...  186 us
    pallas_call x1, Pallas kernels, reduce_weight(): pl.pallas_call(functools.partial(reduce_body, line=line, pairs=pairs, mem...  147 us
  transfers between devices with their start and end apart: 4, of which 0 were waited for; matrix products, arithmetic and copies ran while one was open for 0% of the time, Pallas kernels for 27%

profile of v3, /device:TPU:0, one launch (start us, length us, event | category | flops | bytes accessed | tf_op | source)
XLA Modules:
  0.0 547.1 jit_solution(12728366860779392819)
XLA Ops:
  0.6 186.3 %gather_and_project.1 = (bf16[4096,512]{1,0:T(8,128)(2,1)}, bf16[4096,256]{1,0:T(8,128)(2,1)}, bf16[1024,4096]{1,0:T(8,128)(2,1)}) custom-call(bf16[1024,2048]{1,0:T(8,128)(2,1)} %teacher.1, bf16[1024,1024]{1,0:T(8,128)(2,1)} %hidden.1, bf16[512,1024]{1,0:T(8,128)(2,1)} %weight.1), custom_call_target="tpu_custom_call" | custom-call | tf_op jit(solution)/shard_map/gather_and_project/pallas_call | solution.py:399
  187.0 4.1 copy.6
  191.0 194.6 %relation.1 = (f32[32,256,128]{2,1,0:T(8,128)}, bf16[4096,256]{1,0:T(8,128)(2,1)}) custom-call(bf16[4096,512]{1,0:T(8,128)(2,1)} %get-tuple-element.7.t_keys, bf16[4096,256]{1,0:T(8,128)(2,1)} %get-tuple-element.8.s_keys, bf16[256,4096]{1,0:T(8,128)(2,1)} %bitcast.6), custom_call_target="tpu_custom_call" | custom-call | tf_op jit(solution)/shard_map/relation/pallas_call | solution.py:161
  385.6 3.4 slice_reduce_fusion
  389.0 1.3 collective-permute-start.2
  390.3 0.7 collective-permute-start.3
  391.0 0.7 collective-permute-start
  391.7 4.3 collective-permute-start.1
  396.0 147.2 %reduce_weight.1 = f32[512,1024]{1,0:T(8,128)} custom-call(bf16[1024,4096]{1,0:T(8,128)(2,1)} %get-tuple-element.10.hidden, bf16[4096,256]{1,0:T(8,128)(2,1)} %get-tuple-element.11.grad), custom_call_target="tpu_custom_call" | custom-call | tf_op jit(solution)/shard_map/reduce_weight/pallas_call | solution.py:526
  543.3 0.0 collective-permute-done.2
  543.3 0.0 collective-permute-done.3
  543.3 0.0 collective-permute-done
  543.3 0.0 collective-permute-done.1
  543.3 0.6 pad_maximum_fusion
  543.9 3.2 copy.10
  (4 shorter events, 0.0 us)
Async XLA Ops:
  389.0 154.2 %collective-permute-start.2 = (f32[4096]{0:T(1024)S(1)}, f32[4096]{0:T(1024)S(1)}, u32[]{:S(2)}, u32[]{:S(2)}) collective-permute-start(f32[4096]{0:T(1024)S(1)} %bitcast.10), channel_id=1, source_target_pairs={{4,0},{5,2},{6,4},{7,6},{12,8},{13,10},{14,12},{15,14},{20,16},{21... | collective-permute-start | bytes 49160 | tf_op jit(solution)/shard_map/ppermute | solution.py:558
  390.3 152.9 %collective-permute-start.3 = (f32[4096]{0:T(1024)S(1)}, f32[4096]{0:T(1024)S(1)}, u32[]{:S(2)}, u32[]{:S(2)}) collective-permute-start(f32[4096]{0:T(1024)S(1)} %bitcast.12), channel_id=1, source_target_pairs={{4,1},{5,3},{6,5},{7,7},{12,9},{13,11},{14,13},{15,15},{20,17},{21... | collective-permute-start | bytes 49160 | tf_op jit(solution)/shard_map/ppermute | solution.py:558
  391.0 152.3 %collective-permute-start = (f32[4096]{0:T(1024)S(1)}, f32[4096]{0:T(1024)S(1)}, u32[]{:S(2)}, u32[]{:S(2)}) collective-permute-start(f32[4096]{0:T(1024)S(1)} %bitcast.11), channel_id=1, source_target_pairs={{0,0},{1,2},{2,4},{3,6},{8,8},{9,10},{10,12},{11,14},{16,16},{17,1... | collective-permute-start | bytes 49160 | tf_op jit(solution)/shard_map/ppermute | solution.py:558
  391.7 151.6 %collective-permute-start.1 = (f32[4096]{0:T(1024)S(1)}, f32[4096]{0:T(1024)S(1)}, u32[]{:S(2)}, u32[]{:S(2)}) collective-permute-start(f32[4096]{0:T(1024)S(1)} %bitcast.13), channel_id=1, source_target_pairs={{0,1},{1,3},{2,5},{3,7},{8,9},{9,11},{10,13},{11,15},{16,17},{17,1... | collective-permute-start | bytes 49160 | tf_op jit(solution)/shard_map/ppermute | solution.py:558

commit v4 on v3

--- a/solution.py
+++ b/solution.py
@@ -22,7 +22,6 @@
     )
 
 LOG2E = 1.0 / math.log(2.0)
-LN2 = math.log(2.0)
 LANES = 128
 
 
@@ -64,19 +63,19 @@
         gap = jnp.zeros((group, LANES), jnp.float32)
         for k in range(tiles):
             c = slice(k * LANES, (k + 1) * LANES)
-            u = (t_old[at, c] - t_max) * ct
-            v = (s_old[at, c] - s_max) * cs
-            t_exp = jnp.exp2(u)
-            s_exp = jnp.exp2(v)
+            t_gap = t_old[at, c] - t_max
+            s_gap = s_old[at, c] - s_max
+            t_exp = jnp.exp2(t_gap * ct)
+            s_exp = jnp.exp2(s_gap * cs)
             t_e[:, c] = t_exp
             s_e[:, c] = s_exp
             t_sum = t_sum + t_exp
             s_sum = s_sum + s_exp
-            gap = gap + t_exp * (u - v)
+            gap = gap + t_exp * (t_gap - s_gap * (s_scale / t_scale))
         t_sum = jnp.sum(t_sum, axis=1, keepdims=True)
         s_sum = jnp.sum(s_sum, axis=1, keepdims=True)
         gap = jnp.sum(gap, axis=1, keepdims=True)
-        kl = gap * LN2 / t_sum - jnp.log(t_sum) + jnp.log(s_sum)
+        kl = gap * t_scale / t_sum - jnp.log(t_sum) + jnp.log(s_sum)
         kl_out[0, at, :] = jnp.broadcast_to(kl, (group, LANES))
         return jnp.broadcast_to(1.0 / t_sum, (group, LANES)), jnp.broadcast_to(1.0 / s_sum, (group, LANES))
 

time: 547 us -> 541 us (0.989)
  Pallas kernels: 528 us -> 522 us
    pallas_call x1, Pallas kernels: 195 us -> 188 us  [relation(): pl.pallas_call(functools.partial(relation_body, steps=steps, group=group,...]
where the time goes in v4:
time: 541 us
  Pallas kernels  522 us (96%)
  local copies, waits for them, and re-layouts  10.6 us (2%)
  starting transfers between devices  6.95 us (1%)
    pallas_call x1, Pallas kernels, relation(): pl.pallas_call(functools.partial(relation_body, steps=steps, group=group,...  188 us
    pallas_call x1, Pallas kernels, gather_and_project(): pl.pallas_call(functools.partial(gather_body, line=line, pairs=pairs, mem...  186 us
    pallas_call x1, Pallas kernels, reduce_weight(): pl.pallas_call(functools.partial(reduce_body, line=line, pairs=pairs, mem...  147 us
  transfers between devices with their start and end apart: 4, of which 0 were waited for; matrix products, arithmetic and copies ran while one was open for 0% of the time, Pallas kernels for 27%

profile of v4, /device:TPU:0, one launch (start us, length us, event | category | flops | bytes accessed | tf_op | source)
XLA Modules:
  0.0 540.6 jit_solution(13438155590393327674)
XLA Ops:
  0.6 186.3 %gather_and_project.1 = (bf16[4096,512]{1,0:T(8,128)(2,1)}, bf16[4096,256]{1,0:T(8,128)(2,1)}, bf16[1024,4096]{1,0:T(8,128)(2,1)}) custom-call(bf16[1024,2048]{1,0:T(8,128)(2,1)} %teacher.1, bf16[1024,1024]{1,0:T(8,128)(2,1)} %hidden.1, bf16[512,1024]{1,0:T(8,128)(2,1)} %weight.1), custom_call_target="tpu_custom_call" | custom-call | tf_op jit(solution)/shard_map/gather_and_project/pallas_call | solution.py:398
  187.0 4.1 copy.6
  191.0 188.1 %relation.1 = (f32[32,256,128]{2,1,0:T(8,128)}, bf16[4096,256]{1,0:T(8,128)(2,1)}) custom-call(bf16[4096,512]{1,0:T(8,128)(2,1)} %get-tuple-element.7.t_keys, bf16[4096,256]{1,0:T(8,128)(2,1)} %get-tuple-element.8.s_keys, bf16[256,4096]{1,0:T(8,128)(2,1)} %bitcast.6), custom_call_target="tpu_custom_call" | custom-call | tf_op jit(solution)/shard_map/relation/pallas_call | solution.py:160
  379.1 3.4 slice_reduce_fusion
  382.5 1.3 collective-permute-start.2
  383.8 0.7 collective-permute-start.3
  384.5 0.7 collective-permute-start
  385.2 4.3 collective-permute-start.1
  389.5 147.2 %reduce_weight.1 = f32[512,1024]{1,0:T(8,128)} custom-call(bf16[1024,4096]{1,0:T(8,128)(2,1)} %get-tuple-element.10.hidden, bf16[4096,256]{1,0:T(8,128)(2,1)} %get-tuple-element.11.grad), custom_call_target="tpu_custom_call" | custom-call | tf_op jit(solution)/shard_map/reduce_weight/pallas_call | solution.py:525
  536.7 0.0 collective-permute-done.2
  536.7 0.0 collective-permute-done.3
  536.8 0.0 collective-permute-done
  536.8 0.0 collective-permute-done.1
  536.8 0.6 pad_maximum_fusion
  537.4 3.2 copy.10
  (4 shorter events, 0.0 us)
Async XLA Ops:
  382.5 154.2 %collective-permute-start.2 = (f32[4096]{0:T(1024)S(1)}, f32[4096]{0:T(1024)S(1)}, u32[]{:S(2)}, u32[]{:S(2)}) collective-permute-start(f32[4096]{0:T(1024)S(1)} %bitcast.10), channel_id=1, source_target_pairs={{4,0},{5,2},{6,4},{7,6},{12,8},{13,10},{14,12},{15,14},{20,16},{21... | collective-permute-start | bytes 49160 | tf_op jit(solution)/shard_map/ppermute | solution.py:557
  383.8 152.9 %collective-permute-start.3 = (f32[4096]{0:T(1024)S(1)}, f32[4096]{0:T(1024)S(1)}, u32[]{:S(2)}, u32[]{:S(2)}) collective-permute-start(f32[4096]{0:T(1024)S(1)} %bitcast.12), channel_id=1, source_target_pairs={{4,1},{5,3},{6,5},{7,7},{12,9},{13,11},{14,13},{15,15},{20,17},{21... | collective-permute-start | bytes 49160 | tf_op jit(solution)/shard_map/ppermute | solution.py:557
  384.5 152.3 %collective-permute-start = (f32[4096]{0:T(1024)S(1)}, f32[4096]{0:T(1024)S(1)}, u32[]{:S(2)}, u32[]{:S(2)}) collective-permute-start(f32[4096]{0:T(1024)S(1)} %bitcast.11), channel_id=1, source_target_pairs={{0,0},{1,2},{2,4},{3,6},{8,8},{9,10},{10,12},{11,14},{16,16},{17,1... | collective-permute-start | bytes 49160 | tf_op jit(solution)/shard_map/ppermute | solution.py:557
  385.2 151.6 %collective-permute-start.1 = (f32[4096]{0:T(1024)S(1)}, f32[4096]{0:T(1024)S(1)}, u32[]{:S(2)}, u32[]{:S(2)}) collective-permute-start(f32[4096]{0:T(1024)S(1)} %bitcast.13), channel_id=1, source_target_pairs={{0,1},{1,3},{2,5},{3,7},{8,9},{9,11},{10,13},{11,15},{16,17},{17,1... | collective-permute-start | bytes 49160 | tf_op jit(solution)/shard_map/ppermute | solution.py:557
